TPU v7x, 32 devices: a 4x4x1 block of a 4x4x8 slice. The times are simulated.
32 devices in a mesh: rep: 1 (over z), wg: 32 (over y, x, core).
Axes of the slice: x: 4, y: 4, z: 1, core: 2. Of those that a mesh axis runs over, the one named last changes fastest.
The devices are a block of a 4x4x8 slice.
Arguments:
- x_in: bfloat16 [32, 1024, 3072], P(('rep', 'wg'))
- lengths: int32 [32], P(('rep', 'wg'))
- positions: int32 [32, 1024], P(('rep', 'wg'))
- w_q: bfloat16 [3072, 3072], P('wg')
- w_k: bfloat16 [3072, 1024], P('wg')
- w_v: bfloat16 [3072, 1024], P('wg')
- w_o: bfloat16 [3072, 3072], P('wg')
- w_up: bfloat16 [3072, 9216], P('wg')
- w_down: bfloat16 [9216, 3072], P('wg')
- ln1_gain: float32 [3072], P('wg')
- ln1_bias: float32 [3072], P('wg')
- ln2_gain: float32 [3072], P('wg')
- ln2_bias: float32 [3072], P('wg')
Outputs:
- output 1: bfloat16 [32, 1024, 3072], P(('rep', 'wg'))
- output 2: bfloat16 [32, 1024, 8, 128], P(('rep', 'wg'))
- output 3: bfloat16 [32, 1024, 8, 128], P(('rep', 'wg'))
All inputs are finite; a program needn't handle non-finite values.
Results may differ from a plain program's by a relative error of at most 0.0096177.
Values are sent between devices in bfloat16 or wider.
A program may use at most 768 MiB of HBM per device.

v0:
```python
import jax
import jax.numpy as jnp
from jax import lax
from jax.sharding import PartitionSpec as P

LN_EPS = 1e-5
ROPE_BASE = 10000.0
HEAD_DIM = 128


def layer_norm1p(acts, ln_gain, ln_bias):
    acts_f = acts.astype(jnp.float32)
    row_mean = jnp.mean(acts_f, axis=-1, keepdims=True)
    centered = acts_f - row_mean
    variance = jnp.mean(centered * centered, axis=-1, keepdims=True)
    return (centered * lax.rsqrt(variance + LN_EPS) * (1.0 + ln_gain) + ln_bias).astype(jnp.bfloat16)


def rotary_tables(positions):
    quarter = HEAD_DIM // 4
    inv_freq = ROPE_BASE ** (-jnp.arange(quarter, dtype=jnp.float32) / quarter)
    angles = positions.astype(jnp.float32)[:, :, None, None] * inv_freq
    return jnp.cos(angles), jnp.sin(angles)


def apply_rotary(proj, cos_tab, sin_tab):
    quarter = proj.shape[-1] // 4
    rot_lo = proj[..., :quarter]
    rot_hi = proj[..., quarter:2 * quarter]
    return jnp.concatenate([rot_lo * cos_tab - rot_hi * sin_tab, rot_hi * cos_tab + rot_lo * sin_tab, proj[..., 2 * quarter:]], axis=-1)


def causal_attention(q_grp, k_keep, v_keep, lengths):
    seq_len = q_grp.shape[1]
    score_scale = q_grp.shape[-1] ** -0.5
    q_rows = min(seq_len, 128)
    key_pos = jnp.arange(seq_len)
    key_ok = key_pos[None, :] < lengths[:, None]
    pieces = []
    for block_idx in range(seq_len // q_rows):
        row_lo = block_idx * q_rows
        row_hi = row_lo + q_rows
        scores = jnp.einsum("nqkgd,nskd->nkgqs", q_grp[:, row_lo:row_hi], k_keep[:, :row_hi], preferred_element_type=jnp.float32) * score_scale
        causal = key_pos[None, :row_hi] <= (row_lo + key_pos[:q_rows])[:, None]
        allowed = causal[None, None, None] & key_ok[:, None, None, None, :row_hi]
        scores = jnp.where(allowed, scores, -1e30)
        prob_bf = jax.nn.softmax(scores, axis=-1).astype(jnp.bfloat16)
        att_blk = jnp.einsum("nkgqs,nskd->nqkgd", prob_bf, v_keep[:, :row_hi], preferred_element_type=jnp.float32)
        pieces.append(att_blk.astype(jnp.bfloat16))
    return jnp.concatenate(pieces, axis=1)


def solution(mesh):
    batch_spec = P(("rep", "wg"))
    row_spec = P("wg")

    def gather_rows(part_arr):
        return lax.all_gather(part_arr, "wg", axis=0, tiled=True)

    def local_layer(x_loc, lengths, positions, wq_part, wk_part, wv_part, wo_part, wup_part, wdown_part, gain1_part, bias1_part, gain2_part, bias2_part):
        n_seq, seq_len, d_model = x_loc.shape
        tokens = n_seq * seq_len
        n_heads = wq_part.shape[1] // HEAD_DIM
        n_kv_heads = wk_part.shape[1] // HEAD_DIM
        x_flat = x_loc.reshape(tokens, d_model)
        h_norm = layer_norm1p(x_flat, gather_rows(gain1_part), gather_rows(bias1_part))
        q_acc = jnp.dot(h_norm, gather_rows(wq_part), preferred_element_type=jnp.float32)
        k_acc = jnp.dot(h_norm, gather_rows(wk_part), preferred_element_type=jnp.float32)
        v_acc = jnp.dot(h_norm, gather_rows(wv_part), preferred_element_type=jnp.float32)
        cos_tab, sin_tab = rotary_tables(positions)
        tok_valid = (jnp.arange(seq_len)[None, :] < lengths[:, None])[:, :, None, None]
        q_grp = apply_rotary(q_acc.reshape(n_seq, seq_len, n_heads, HEAD_DIM), cos_tab, sin_tab).astype(jnp.bfloat16).reshape(n_seq, seq_len, n_kv_heads, n_heads // n_kv_heads, HEAD_DIM)
        k_keep = jnp.where(tok_valid, apply_rotary(k_acc.reshape(n_seq, seq_len, n_kv_heads, HEAD_DIM), cos_tab, sin_tab).astype(jnp.bfloat16), 0)
        v_keep = jnp.where(tok_valid, v_acc.reshape(n_seq, seq_len, n_kv_heads, HEAD_DIM).astype(jnp.bfloat16), 0)
        att_flat = causal_attention(q_grp, k_keep, v_keep, lengths).reshape(tokens, n_heads * HEAD_DIM)
        o_acc = jnp.dot(att_flat, gather_rows(wo_part), preferred_element_type=jnp.float32)
        x_mid = (x_flat.astype(jnp.float32) + o_acc).astype(jnp.bfloat16)
        h_mid = layer_norm1p(x_mid, gather_rows(gain2_part), gather_rows(bias2_part))
        up_acc = jnp.dot(h_mid, gather_rows(wup_part), preferred_element_type=jnp.float32)
        sq_relu = jnp.square(jnp.maximum(up_acc, 0.0)).astype(jnp.bfloat16)
        down_acc = jnp.dot(sq_relu, gather_rows(wdown_part), preferred_element_type=jnp.float32)
        y_out = (x_mid.astype(jnp.float32) + down_acc).astype(jnp.bfloat16)
        return y_out.reshape(n_seq, seq_len, d_model), k_keep, v_keep

    return jax.shard_map(local_layer, mesh=mesh, in_specs=(batch_spec, batch_spec, batch_spec) + (row_spec,) * 10, out_specs=(batch_spec, batch_spec, batch_spec), check_vma=False)
```

profile of v0, /device:TPU:97, one launch (start us, length us, event | category | flops | bytes accessed | tf_op | source)
XLA Modules:
  0.0 666.3 jit_solution(2550350233425420322)
XLA Ops:
  15.1 50.9 %all-reduce.4 = (f32[3072]{0:T(1024)S(1)}, f32[3072]{0:T(1024)S(1)}, f32[3072]{0:T(1024)}, f32[3072]{0:T(1024)S(1)}) all-reduce(f32[3072]{0:T(1024)S(1)} %dynamic-update-slice.1, f32[3072]{0:T(1024)S(1)} %dynamic-update-slice, f32[3072]{0:T(1024)S(1)} %dynamic-update-slice.3, ...), channel_id=1, replica_groups=mesh['rep'=1,'wg'=32] {'wg'}, use_global_device_ids=true, to_apply=%add.1 | all-reduce | flops 12288 | bytes 98304
  66.2 3.8 convert_reduce_fusion.1
  70.6 1.8 fusion.11
  78.4 8.6 %copy.56 = bf16[1024,3072]{1,0:T(8,128)(2,1)} copy(bf16[1024,3072]{0,1:T(8,128)(2,1)} %bitcast.493) | data formatting | bytes 12582912 | tf_op jit(solution)/shard_map/dot_general | solution.py:68
  87.0 10.7 %convolution_bitcast_fusion.1 = f32[1,1024,8,128]{3,1,2,0:T(8,128)S(1)} fusion(bf16[8,128,3072]{2,1,0:T(8,128)(2,1)} %bitcast.497, bf16[1,1024,3072]{2,1,0:T(8,128)(2,1)} %param.13, f32[3072]{0:T(1024)S(1)} %get-tuple-element.12, f32[3072]{0:T(1024)S(1)} %broadcast_add_fusion.1, f32[1024]{0:T(1024)S(1)} %add_rsqrt_fusion.1, ...), kind=kOutput, calls=%fused_computation.92 | convolution fusion | flops 6461325312 | bytes 16809984 | tf_op jit(solution)/shard_map/dot_general | solution.py:68
  97.8 2.0 copy-done
  99.8 1.9 slice.332
  103.1 8.9 %copy.55 = bf16[1024,3072]{1,0:T(8,128)(2,1)} copy(bf16[1024,3072]{0,1:T(8,128)(2,1)} %bitcast.494) | data formatting | bytes 12582912 | tf_op jit(solution)/shard_map/dot_general | solution.py:69
  112.0 5.0 subtract_convert_fusion
  117.2 2.2 maximum_select_fusion
  119.4 2.7 copy.73
  123.0 7.4 %convert_select_fusion = bf16[1024,8,128]{2,0,1:T(8,128)(2,1)S(1)} fusion(pred[1024]{0:T(1024)(128)(4,1)S(1)} %copy-done.42, bf16[8,128,3072]{2,1,0:T(8,128)(2,1)S(1)} %bitcast.495, bf16[1,1024,3072]{2,1,0:T(8,128)(2,1)S(1)} %bitcast.485, f32[3072]{0:T(1024)S(1)} %copy-done.48, f32[3072]{0:T(1024)S(1)} %copy-done.40, f32[1024]{0:T(1024)S(1)} %copy-done.45, ...), kind=kOutput, calls=%fused_computation.102 | convolution fusion | flops 6463422464 | bytes 14713856 | tf_op jit(solution)/shard_map/dot_general | solution.py:69
  131.7 2.7 copy.74
  134.4 1.9 slice_bitcast_fusion.61
  136.3 39.9 %all-gather.11.cloned.1.call-done = bf16[3072,3072]{1,0:T(8,128)(2,1)} async-done(((bf16[96,3072]{1,0:T(8,128)(2,1)}), bf16[3072,3072]{1,0:T(8,128)(2,1)}) %all-gather.11.cloned.1.call-update) | async-done | bytes 18874384 | tf_op jit(solution)/shard_map/all_gather | solution.py:58
  176.1 24.6 %copy.60 = bf16[3072,3072]{1,0:T(8,128)(2,1)} copy(bf16[3072,3072]{0,1:T(8,128)(2,1)} %bitcast.486) | data formatting | bytes 37748736 | tf_op jit(solution)/shard_map/dot_general | solution.py:67
  200.8 25.7 %convolution_bitcast_fusion = f32[1,1024,24,128]{1,3,2,0:T(8,128)S(1)} fusion(bf16[24,128,3072]{2,1,0:T(8,128)(2,1)} %bitcast.487, bf16[1,1024,3072]{2,1,0:T(8,128)(2,1)} %param.13, f32[3072]{0:T(1024)S(1)} %copy-done.48, f32[3072]{0:T(1024)S(1)} %copy-done.40, f32[1024]{0:T(1024)S(1)} %copy-done.45, f32[1024]{0:T(1024)S(1)} %copy-done.36), kind=kOutput, calls=%fused_computation.70 | convolution fusion | flops 19346227200 | bytes 37781504 | tf_op jit(solution)/shard_map/dot_general | solution.py:67
  226.9 2.8 subtract_convert_fusion.1
  229.7 6.4 copy.61
  236.1 6.3 copy.62
  242.4 4.5 copy.63
  246.8 9.9 %pad_maximum_fusion = bf16[1,1024,8,3,128]{4,1,3,2,0:T(8,128)(2,1)S(1)} fusion(bf16[1,1024,8,3,64]{4,1,3,2,0:T(8,128)(2,1)} %copy.63, bf16[1,1024,8,3,32]{4,1,3,2,0:T(8,128)(2,1)} %copy.62, bf16[1,1024,8,3,32]{4,1,3,2,0:T(8,128)(2,1)} %copy.61), kind=kLoop, calls=%fused_computation.47 | loop fusion | flops 18874368 | bytes 12582912 | tf_op jit(solution)/shard_map/concatenate | solution.py:30
  259.5 2.3 fusion.104
  263.3 1.6 fusion.51
  267.4 1.4 copy-done.12
  268.7 2.6 fusion.43
  271.3 1.5 fusion.23
  272.9 6.3 fusion.21
  279.2 2.5 fusion.24
  281.6 3.2 fusion.126
  284.8 5.0 fusion.20
  289.9 2.0 fusion.22
  291.9 6.5 fusion.19
  298.4 2.9 fusion.120
  301.4 2.6 fusion.18
  304.0 5.8 fusion.114
  309.9 6.6 fusion.108
  316.5 4.2 fusion.148
  320.8 8.3 %fusion.142 = bf16[1,1024,8,3,128]{4,1,3,2,0:T(8,128)(2,1)} fusion(bf16[1,1024,8,3,128]{4,1,3,2,0:T(8,128)(2,1)} %fusion.148, f32[8,3,128]{2,1,0:T(4,128)S(1)} %fusion.19, f32[8,3,128]{2,1,0:T(4,128)S(1)} %get-tuple-element.42, f32[8,896,128,3]{2,1,3,0:T(8,128)} %get-tuple-element.43, pred[128,896]{0,1:T(8,128)(4,1)S(1)} %compare_and_fusion, ...), kind=kOutput, calls=%fused_computation.141 | convolution fusion | flops 718798848 | bytes 13778944 | tf_op jit(solution)/shard_map/nkgqs,nskd->nqkgd/dot_general | solution.py:48
  329.1 5.4 fusion.134
  334.6 8.7 %copy.72 = bf16[1,1024,8,3,128]{1,4,3,2,0:T(8,128)(2,1)} copy(bf16[1,1024,8,3,128]{4,1,3,2,0:T(8,128)(2,1)} %fusion.134) | data formatting | bytes 12582912 | tf_op jit(solution)/shard_map/concatenate | solution.py:50
  343.2 26.1 %convert_reduce_fusion = (f32[1024]{0:T(1024)S(1)}, bf16[1024,3072]{1,0:T(8,128)(2,1)S(1)}) fusion(bf16[1024,3072]{0,1:T(8,128)(2,1)} %bitcast.496, bf16[3072,3072]{1,0:T(8,128)(2,1)} %all-gather.13.cloned.1.call-done, bf16[1,1024,3072]{2,1,0:T(8,128)(2,1)} %param.13), kind=kOutput, calls=%fused_computation.4 | convolution fusion | flops 19343081472 | bytes 37752832 | tf_op jit(solution)/shard_map/dot_general | solution.py:76
  369.4 2.7 copy-done.13
  372.1 1.8 fusion.6
  373.8 45.9 %all-gather.15.cloned.1.call-done = bf16[3072,9216]{1,0:T(8,128)(2,1)} async-done(((bf16[96,9216]{1,0:T(8,128)(2,1)}), bf16[3072,9216]{1,0:T(8,128)(2,1)}) %all-gather.15.cloned.1.call-update) | async-done | bytes 56623120 | tf_op jit(solution)/shard_map/all_gather | solution.py:58
  419.7 66.8 %multiply_convert_fusion.clone.6 = bf16[1024,9216]{1,0:T(8,128)(2,1)} fusion(bf16[3072,9216]{1,0:T(8,128)(2,1)} %all-gather.15.cloned.1.call-done, bf16[1024,3072]{1,0:T(8,128)(2,1)} %copy-done.13, f32[3072]{0:T(1024)S(1)} %copy-done.46, f32[3072]{0:T(1024)S(1)} %copy-done.38, f32[1024]{0:T(1024)S(1)} %add_rsqrt_fusion, ...), kind=kOutput, calls=%fused_computation.clone.clone.clone.clone.clone.1 | convolution fusion | flops 58029244416 | bytes 81821696 | tf_op jit(solution)/shard_map/dot_general | solution.py:79
  486.5 102.7 %all-gather.17.cloned.1.call-done = bf16[9216,3072]{1,0:T(8,128)(2,1)} async-done(((bf16[288,3072]{1,0:T(8,128)(2,1)}), bf16[9216,3072]{1,0:T(8,128)(2,1)}) %all-gather.17.cloned.1.call-update) | async-done | bytes 56623120 | tf_op jit(solution)/shard_map/all_gather | solution.py:58
  589.2 70.0 %fusion.25 = bf16[1,1024,3072]{2,1,0:T(8,128)(2,1)} fusion(bf16[1024,3072]{1,0:T(8,128)(2,1)} %copy-done.13, bf16[9216,3072]{1,0:T(8,128)(2,1)} %all-gather.17.cloned.1.call-done, bf16[1024,9216]{1,0:T(8,128)(2,1)} %multiply_convert_fusion.clone.6), kind=kOutput, calls=%fused_computation.44 | convolution fusion | flops 57991495680 | bytes 88080384 | tf_op jit(solution)/shard_map/dot_general | solution.py:81
  (190 shorter events, 24.4 us)
Async XLA Ops:
  7.2 6.8 %copy-start.49 = (f32[96]{0:T(128)S(1)}, f32[96]{0:T(128)}, u32[]{:S(2)}) copy-start(f32[96]{0:T(128)} %param.22) | copy-start | bytes 1156
  7.2 7.0 %copy-start.50 = (f32[96]{0:T(128)S(1)}, f32[96]{0:T(128)}, u32[]{:S(2)}) copy-start(f32[96]{0:T(128)} %param.23) | copy-start | bytes 1156
  7.2 7.3 %copy-start.51 = (f32[96]{0:T(128)S(1)}, f32[96]{0:T(128)}, u32[]{:S(2)}) copy-start(f32[96]{0:T(128)} %param.24) | copy-start | bytes 1156
  7.2 7.6 %copy-start.52 = (f32[96]{0:T(128)S(1)}, f32[96]{0:T(128)}, u32[]{:S(2)}) copy-start(f32[96]{0:T(128)} %param.25) | copy-start | bytes 1156
  7.2 71.2 %all-gather.9.cloned.1.call-start = ((), (), s32[]{:S(2)}) async-start(), calls=%async_computation.1 | async-start | bytes 6488064 | tf_op jit(solution)/shard_map/all_gather | solution.py:58
  8.0 95.0 %all-gather.7.cloned.1.call-start = ((), (), s32[]{:S(2)}) async-start(), calls=%async_computation | async-start | bytes 6488064 | tf_op jit(solution)/shard_map/all_gather | solution.py:58
  8.8 167.3 %all-gather.11.cloned.1.call-start = ((), (), s32[]{:S(2)}) async-start(), calls=%async_computation.2 | async-start | bytes 19464192 | tf_op jit(solution)/shard_map/all_gather | solution.py:58
  9.6 333.6 %all-gather.13.cloned.1.call-start = ((), (), s32[]{:S(2)}) async-start(), calls=%async_computation.3 | async-start | bytes 19464192 | tf_op jit(solution)/shard_map/all_gather | solution.py:58
  10.3 409.4 %all-gather.15.cloned.1.call-start = ((), (), s32[]{:S(2)}) async-start(), calls=%async_computation.4 | async-start | bytes 58392576 | tf_op jit(solution)/shard_map/all_gather | solution.py:58
  10.9 578.3 %all-gather.17.cloned.1.call-start = ((), (), s32[]{:S(2)}) async-start(), calls=%async_computation.5 | async-start | bytes 58392576 | tf_op jit(solution)/shard_map/all_gather | solution.py:58
  66.0 21.1 %copy-start.47 = (f32[3072]{0:T(1024)}, f32[3072]{0:T(1024)S(1)}, u32[]{:S(2)}) copy-start(f32[3072]{0:T(1024)S(1)} %get-tuple-element.12) | copy-start | bytes 36868
  66.0 4.6 copy-start.2
  66.0 11.6 %copy-start.41 = (pred[1024]{0:T(1024)(128)(4,1)}, pred[1024]{0:T(1024)(128)(4,1)S(1)}, u32[]{:S(2)}) copy-start(pred[1024]{0:T(1024)(128)(4,1)S(1)} %iota_compare_fusion.2) | copy-start | bytes 3076
  70.6 16.5 %copy-start.35 = (f32[1024]{0:T(1024)}, f32[1024]{0:T(1024)S(1)}, u32[]{:S(2)}) copy-start(f32[1024]{0:T(1024)S(1)} %broadcast_multiply_fusion.1) | copy-start | bytes 12292
  72.4 14.7 %copy-start.44 = (f32[1024]{0:T(1024)}, f32[1024]{0:T(1024)S(1)}, u32[]{:S(2)}) copy-start(f32[1024]{0:T(1024)S(1)} %add_rsqrt_fusion.1) | copy-start | bytes 12292
  73.1 13.9 %copy-start.39 = (f32[3072]{0:T(1024)}, f32[3072]{0:T(1024)S(1)}, u32[]{:S(2)}) copy-start(f32[3072]{0:T(1024)S(1)} %broadcast_add_fusion.1) | copy-start | bytes 36868
  103.1 19.0 %slice-start = ((s8[6291456]{0:T(1024)(128)(4,1)}), s8[2097152]{0:T(1024)(128)(4,1)S(1)}, s32[]{:S(2)}) async-start(s8[6291456]{0:T(1024)(128)(4,1)} %bitcast.484), calls=%async_computation.6 | async-start | bytes 4194304
  112.0 5.1 copy-start.6
  112.0 5.1 copy-start.42
  112.0 10.0 %slice-start.1 = ((s8[6291456]{0:T(1024)(128)(4,1)}), s8[4194304]{0:T(1024)(128)(4,1)S(1)}, s32[]{:S(2)}) async-start(s8[6291456]{0:T(1024)(128)(4,1)} %bitcast.484), calls=%async_computation.7 | async-start | bytes 8388608
  117.1 5.0 copy-start.7
  117.1 5.0 copy-start.9
  117.1 5.8 copy-start.14
  117.2 5.8 copy-start.36
  117.2 5.8 copy-start.40
  117.2 5.8 copy-start.45
  117.2 5.8 copy-start.48
  123.0 11.4 %copy-start.1 = (f32[1,1024,8,128]{3,1,2,0:T(8,128)S(1)}, f32[1,1024,8,128]{3,1,2,0:T(8,128)}, u32[]{:S(2)}) copy-start(f32[1,1024,8,128]{3,1,2,0:T(8,128)} %copy-done) | copy-start | bytes 12582916
  246.8 9.9 %copy-start.5 = (bf16[1,1024,8,128]{3,1,2,0:T(8,128)(2,1)S(1)}, bf16[1,1024,8,128]{3,1,2,0:T(8,128)(2,1)}, u32[]{:S(2)}) copy-start(bf16[1,1024,8,128]{3,1,2,0:T(8,128)(2,1)} %copy-done.4) | copy-start | bytes 6291460
  246.8 9.9 %copy-start.37 = (pred[128,128]{0,1:T(8,128)(4,1)S(1)}, pred[128,128]{0,1:T(8,128)(4,1)}, u32[]{:S(2)}) copy-start(pred[128,128]{0,1:T(8,128)(4,1)} %compare_and_fusion.6) | copy-start | bytes 49156
  256.8 16.1 %copy-start.15 = (bf16[1,1024,8,3,128]{4,1,3,2,0:T(8,128)(2,1)}, bf16[1,1024,8,3,128]{4,1,3,2,0:T(8,128)(2,1)S(1)}, u32[]{:S(2)}) copy-start(bf16[1,1024,8,3,128]{4,1,3,2,0:T(8,128)(2,1)S(1)} %pad_maximum_fusion) | copy-start | bytes 18874372
  258.2 3.6 copy-start.24
  262.7 3.3 copy-start.16
  266.0 5.3 copy-start.25
  266.0 5.3 copy-start.21
  267.4 11.8 %copy-start.11 = (f32[8,640,128,3]{2,1,3,0:T(8,128)}, f32[8,640,128,3]{2,1,3,0:T(8,128)S(1)}, u32[]{:S(2)}) copy-start(f32[8,640,128,3]{2,1,3,0:T(8,128)S(1)} %get-tuple-element.39) | copy-start | bytes 23592964
  272.9 17.0 %copy-start.3 = (f32[8,768,128,3]{2,1,3,0:T(8,128)}, f32[8,768,128,3]{2,1,3,0:T(8,128)S(1)}, u32[]{:S(2)}) copy-start(f32[8,768,128,3]{2,1,3,0:T(8,128)S(1)} %get-tuple-element.41) | copy-start | bytes 28311556
  291.8 6.6 slice-start.5
  291.8 6.6 copy-start.18
  291.9 6.6 copy-start.28
  291.9 6.6 copy-start.29
  291.9 6.6 slice-start.6
  304.0 5.9 copy-start.31
  304.0 12.5 %slice-start.2 = ((s8[9437184]{0:T(1024)(128)(4,1)}), s8[4194304]{0:T(1024)(128)(4,1)S(1)}, s32[]{:S(2)}) async-start(s8[9437184]{0:T(1024)(128)(4,1)} %bitcast.489), calls=%async_computation.8 | async-start | bytes 8388608
  304.0 12.5 %slice-start.3 = ((s8[9437184]{0:T(1024)(128)(4,1)}), s8[4194304]{0:T(1024)(128)(4,1)S(1)}, s32[]{:S(2)}) async-start(s8[9437184]{0:T(1024)(128)(4,1)} %bitcast.489), calls=%async_computation.9 | async-start | bytes 8388608
  309.9 6.7 slice-start.4
  369.4 50.3 %copy-start.38 = (f32[3072]{0:T(1024)S(1)}, f32[3072]{0:T(1024)}, u32[]{:S(2)}) copy-start(f32[3072]{0:T(1024)} %broadcast_add_fusion) | copy-start | bytes 36868
  369.4 50.3 %copy-start.46 = (f32[3072]{0:T(1024)S(1)}, f32[3072]{0:T(1024)}, u32[]{:S(2)}) copy-start(f32[3072]{0:T(1024)} %get-tuple-element.14) | copy-start | bytes 36868
  (18 other events, 45.3 us)
Sparse Core Ops, SparseCore 0:
  10.1 48.2 all-gather.8
  60.5 42.5 all-gather.6
  105.1 70.9 all-gather.10
  178.1 71.6 all-gather.12
  251.7 167.9 all-gather.14
  421.6 167.5 all-gather.16
where the time goes:
time: 671 us; the launch traced here: 666 us
  matrix products  263 us (39%)
  waiting for transfers between devices  194 us (29%)
  local copies, waits for them, and re-layouts  88.9 us (13%)
  other arithmetic  53.8 us (8%)
  blocking collectives  50.9 us (8%)
  between operations  15.9 us (2%)
    all_gather x6, waiting for transfers between devices, gather_rows(): return lax.all_gather(part_arr, 'wg', axis=0, tiled=True)  190 us
    dot_general x1, matrix products, local_layer(): jnp.dot(sq_relu, gather_rows(wdown_part), preferred_element_type=jnp.floa...  70 us
    dot_general x1, matrix products, local_layer(): jnp.dot(h_mid, gather_rows(wup_part), preferred_element_type=jnp.float32)  66.8 us
    unnamed x1, blocking collectives  50.9 us
    dot_general x8, matrix products, causal_attention(): jnp.einsum('nkgqs,nskd->nqkgd', prob_bf, v_keep[:, :row_hi], preferred_el...  38.9 us
    dot_general x1, matrix products, local_layer(): jnp.dot(att_flat, gather_rows(wo_part), preferred_element_type=jnp.float32)  26.1 us
    dot_general x1, matrix products, local_layer(): jnp.dot(h_norm, gather_rows(wq_part), preferred_element_type=jnp.float32)  25.7 us
    dot_general x1, local copies, waits for them, and re-layouts, local_layer(): jnp.dot(h_norm, gather_rows(wq_part), preferred_element_type=jnp.float32)  24.6 us
  transfers between devices with their start and end apart: 6, of which 4 were waited for; matrix products, arithmetic and copies ran while one was open for 49% of the time, Pallas kernels for 0%

commit v1 on v0

v1 whole, which is shorter than its diff:
```python
import functools
import math

import jax
import jax.numpy as jnp
from jax import lax
from jax.experimental import pallas as pl
from jax.experimental.pallas import tpu as pltpu
from jax.sharding import PartitionSpec as P

LN_EPS = 1e-5
ROPE_BASE = 10000.0
HEAD_DIM = 128
LANES = 128
MESH = pl.DeviceIdType.MESH
F32 = jnp.float32
BF16 = jnp.bfloat16


def rotary_tables(positions):
    quarter = HEAD_DIM // 4
    inv_freq = ROPE_BASE ** (-jnp.arange(quarter, dtype=F32) / quarter)
    angles = positions.astype(F32)[:, None] * inv_freq
    cos, sin = jnp.cos(angles), jnp.sin(angles)
    pad = jnp.zeros((positions.shape[0], 2 * quarter), F32)
    return jnp.concatenate([cos, cos, pad], axis=1), jnp.concatenate([-sin, sin, pad], axis=1)


def layer_kernel(cfg, len_ref, cos_ref, sin_ref, x_ref, ln_ref, wq_ref, wk_ref, wv_ref, wo_ref, wu_ref, wd_ref,
                 y_ref, k_out, v_out, gln, gq, gk, gv, go, gu, gd,
                 x_s, h_s, q_s, k_s, v_s, a_s, wb, wbd, acc_s, lnv, lnbuf, lnst,
                 send_sem, recv_sem, stage_sem, own_sem, wb_sem, wbd_sem, io_sem):
    side = cfg["side"]
    seq, d_model = x_s.shape
    n_heads, n_kv = q_s.shape[0], k_s.shape[0]
    tile, rows_m = cfg["tile"], cfg["rows_m"]
    me = lax.axis_index("wg")
    c = lax.rem(me, 2)
    x = lax.rem(me // 2, side)
    y = me // (2 * side)
    xp, xm = lax.rem(x + 1, side), lax.rem(x + side - 1, side)
    yp, ym = lax.rem(y + 1, side), lax.rem(y + side - 1, side)
    xo, yo = lax.rem(x + 2, side), lax.rem(y + 2, side)

    def device(yy, xx, cc):
        return (yy * side + xx) * 2 + cc

    d_xp, d_xm, d_yp, d_ym = device(y, xp, c), device(y, xm, c), device(yp, x, c), device(ym, x, c)
    d_peer = device(y, x, 1 - c)

    barrier = pltpu.get_barrier_semaphore()
    for dev in (d_xp, d_xm, d_yp, d_ym, d_peer):
        pl.semaphore_signal(barrier, inc=1, device_id={"wg": dev}, device_id_type=MESH)
    pl.semaphore_wait(barrier, 5)

    shards = {"ln": (ln_ref, gln), "q": (wq_ref, gq), "k": (wk_ref, gk), "v": (wv_ref, gv), "o": (wo_ref, go),
              "u": (wu_ref, gu), "d": (wd_ref, gd)}
    blocks = cfg["blocks"]

    def put(blk, phase, src, dst, dev):
        pltpu.make_async_remote_copy(
            src_ref=src, dst_ref=dst, send_sem=send_sem.at[blk, phase], recv_sem=recv_sem.at[blk, phase],
            device_id={"wg": dev}, device_id_type=MESH).start()

    def same(blk, phase, ref, dev):
        put(blk, phase, ref, ref, dev)

    def cols_of(blk):
        name, c0, width = blocks[blk]
        half, quarter = width // 2, width // 4
        return (pl.ds(c0, half), pl.ds(c0, quarter), pl.ds(c0 + quarter, quarter),
                pl.ds(c0 + half, half), pl.ds(c0 + half, quarter), pl.ds(c0 + half + quarter, quarter), pl.ds(c0, width))

    def unit_refs(blk):
        name, c0, width = blocks[blk]
        g = shards[name][1]
        cw = pl.ds(c0, width)
        return (g.at[0, pl.ds(0, 2), 0, :, cw], g.at[0, 0, 0, :, cw], g.at[0, :, :, :, cw],
                g.at[0, :, 0, :, cw], g.at[:, :, 0, :, cw])

    def wait_on(ref, sem):
        pltpu.make_async_copy(ref, ref, sem).wait()

    def wait_recv(blk, phase):
        wait_on(unit_refs(blk)[phase], recv_sem.at[blk, phase])

    def wait_send(blk):
        for phase, ref in enumerate(unit_refs(blk)):
            wait_on(ref, send_sem.at[blk, phase])

    def phase_1a(blk):
        w, g = shards[blocks[blk][0]]
        ca, _, _, cb, _, _, cw = cols_of(blk)
        put(blk, 0, w.at[:, ca], g.at[y, x, c, :, ca], d_xp)
        put(blk, 0, w.at[:, ca], g.at[y, x, c, :, ca], d_xm)
        put(blk, 0, w.at[:, cb], g.at[y, x, c, :, cb], d_yp)
        put(blk, 0, w.at[:, cb], g.at[y, x, c, :, cb], d_ym)
        put(blk, 4, w.at[:, cw], g.at[y, x, c, :, cw], d_peer)

    def phase_1b(blk):
        g = shards[blocks[blk][0]][1]
        ca, a0, a1, cb, b0, b1, _ = cols_of(blk)
        wait_recv(blk, 0)
        same(blk, 1, g.at[y, xm, c, :, a0], d_xp)
        same(blk, 1, g.at[y, xp, c, :, a1], d_xm)
        same(blk, 1, g.at[ym, x, c, :, b0], d_yp)
        same(blk, 1, g.at[yp, x, c, :, b1], d_ym)
        same(blk, 4, g.at[y, xm, c, :, ca], d_peer)
        same(blk, 4, g.at[y, xp, c, :, ca], d_peer)
        same(blk, 4, g.at[ym, x, c, :, cb], d_peer)
        same(blk, 4, g.at[yp, x, c, :, cb], d_peer)

    def phase_2a(blk):
        g = shards[blocks[blk][0]][1]
        ca, _, _, cb, _, _, _ = cols_of(blk)
        wait_recv(blk, 1)
        same(blk, 2, g.at[y, :, c, :, ca], d_yp)
        same(blk, 2, g.at[y, :, c, :, ca], d_ym)
        same(blk, 2, g.at[:, x, c, :, cb], d_xp)
        same(blk, 2, g.at[:, x, c, :, cb], d_xm)
        same(blk, 4, g.at[y, xo, c, :, ca], d_peer)
        same(blk, 4, g.at[yo, x, c, :, cb], d_peer)

    def phase_2b(blk):
        g = shards[blocks[blk][0]][1]
        ca, a0, a1, cb, b0, b1, _ = cols_of(blk)
        same(blk, 3, g.at[ym, :, c, :, a0], d_yp)
        same(blk, 3, g.at[yp, :, c, :, a1], d_ym)
        same(blk, 3, g.at[:, xm, c, :, b0], d_xp)
        same(blk, 3, g.at[:, xp, c, :, b1], d_xm)
        same(blk, 4, g.at[ym, :, c, :, ca], d_peer)
        same(blk, 4, g.at[yp, :, c, :, ca], d_peer)
        same(blk, 4, g.at[:, xm, c, :, cb], d_peer)
        same(blk, 4, g.at[:, xp, c, :, cb], d_peer)

    def finish(blk):
        g = shards[blocks[blk][0]][1]
        ca, _, _, cb, _, _, _ = cols_of(blk)
        wait_recv(blk, 3)
        same(blk, 4, g.at[yo, :, c, :, ca], d_peer)
        same(blk, 4, g.at[:, xo, c, :, cb], d_peer)

    def ready(blk):
        wait_recv(blk, 4)

    n_blk = len(blocks)

    def service(j):
        wait_recv(j, 2)
        if j + 1 < n_blk:
            phase_2a(j + 1)
        phase_2b(j)
        if j + 3 < n_blk:
            phase_1b(j + 3)
        if j + 5 < n_blk:
            phase_1a(j + 5)

    def matmul_tiles(g, col0, n_tiles, epilogue):
        def fetch(t, slot):
            return pltpu.make_async_copy(
                g.at[:, :, :, :, pl.ds(pl.multiple_of(col0 + t * tile, LANES), tile)], wb.at[slot], wb_sem.at[slot])

        fetch(0, 0).start()

        @pl.loop(0, n_tiles)
        def _(t):
            slot = lax.rem(t, 2)

            @pl.when(t + 1 < n_tiles)
            def _():
                fetch(t + 1, lax.rem(t + 1, 2)).start()

            fetch(t, slot).wait()

            @pl.loop(0, seq // rows_m)
            def _(m):
                rows = pl.ds(pl.multiple_of(m * rows_m, rows_m), rows_m)
                weights = wb[slot].reshape(d_model, tile)
                epilogue(t, rows, m, jnp.dot(h_s[rows, :], weights, preferred_element_type=F32))

    lane = lax.broadcasted_iota(jnp.int32, (rows_m, HEAD_DIM), 1)
    eighth = HEAD_DIM // 4

    def rotate(vals, rows):
        swapped = jnp.where(lane < eighth, pltpu.roll(vals, HEAD_DIM - eighth, 1), pltpu.roll(vals, eighth, 1))
        turned = vals * cos_ref[rows, :] + swapped * sin_ref[rows, :]
        return jnp.where(lane < 2 * eighth, turned, vals)

    heads_per_tile = tile // HEAD_DIM
    length = len_ref[0]

    def q_tiles(col0, width):
        def epilogue(t, rows, m, acc):
            for i in range(heads_per_tile):
                part = acc[:, i * HEAD_DIM:(i + 1) * HEAD_DIM]
                q_s[col0 // HEAD_DIM + t * heads_per_tile + i, rows, :] = rotate(part, rows).astype(BF16)

        matmul_tiles(gq, col0, width // tile, epilogue)

    def kv_tiles(g, out, turn, width):
        def epilogue(t, rows, m, acc):
            token = m * rows_m + lax.broadcasted_iota(jnp.int32, (rows_m, HEAD_DIM), 0)
            for i in range(heads_per_tile):
                part = acc[:, i * HEAD_DIM:(i + 1) * HEAD_DIM]
                part = rotate(part, rows) if turn else part
                kept = jnp.where(token < length, part, 0.0).astype(BF16)
                out[t * heads_per_tile + i, rows, :] = kept

        matmul_tiles(g, 0, width // tile, epilogue)

    per_kv = n_heads // n_kv
    q_rows = cfg["q_rows"]
    score_scale = HEAD_DIM ** -0.5

    def attention(g_lo, g_hi):
        @pl.loop(g_lo, g_hi)
        def _(kv):
            for blk in range(seq // q_rows):
                lo, hi = blk * q_rows, (blk + 1) * q_rows
                key = lax.broadcasted_iota(jnp.int32, (q_rows, hi), 1)
                query = lo + lax.broadcasted_iota(jnp.int32, (q_rows, hi), 0)
                allowed = (key <= query) & (key < length)
                for i in range(per_kv):
                    head = kv * per_kv + i
                    scores = lax.dot_general(q_s[head, lo:hi, :], k_s[kv, :hi, :], (((1,), (1,)), ((), ())),
                                             preferred_element_type=F32) * score_scale
                    scores = jnp.where(allowed, scores, -1e30)
                    probs = jnp.exp(scores - jnp.max(scores, axis=1, keepdims=True))
                    probs = probs * (1.0 / jnp.sum(probs, axis=1, keepdims=True))
                    out = jnp.dot(probs.astype(BF16), v_s[kv, :hi, :], preferred_element_type=F32)
                    h_s[lo:hi, pl.ds(pl.multiple_of(head * HEAD_DIM, HEAD_DIM), HEAD_DIM)] = out.astype(BF16)

    def o_tiles(col0, width):
        def epilogue(t, rows, m, acc):
            cols = pl.ds(pl.multiple_of(col0 + t * tile, LANES), tile)
            x_s[rows, cols] = (x_s[rows, cols].astype(F32) + acc).astype(BF16)

        matmul_tiles(go, col0, width // tile, epilogue)

    def up_tiles(col0, width):
        def epilogue(t, rows, m, acc):
            cols = pl.ds(pl.multiple_of(col0 + t * tile, LANES), tile)
            a_s[rows, cols] = jnp.square(jnp.maximum(acc, 0.0)).astype(BF16)

        matmul_tiles(gu, col0, width // tile, epilogue)

    def down_tile(col0):
        cols = pl.ds(col0, tile)
        depth = a_s.shape[1] // side

        def fetch(k, slot):
            return pltpu.make_async_copy(gd.at[k, :, :, :, cols], wbd.at[slot], wbd_sem.at[slot])

        fetch(0, 0).start()

        @pl.loop(0, side)
        def _(k):
            slot = lax.rem(k, 2)

            @pl.when(k + 1 < side)
            def _():
                fetch(k + 1, lax.rem(k + 1, 2)).start()

            fetch(k, slot).wait()
            deep = pl.ds(pl.multiple_of(k * depth, LANES), depth)

            @pl.loop(0, seq // rows_m)
            def _(m):
                rows = pl.ds(pl.multiple_of(m * rows_m, rows_m), rows_m)
                part = jnp.dot(a_s[rows, deep], wbd[slot].reshape(depth, tile), preferred_element_type=F32)
                acc_s[rows, :] = jnp.where(k == 0, part, acc_s[rows, :] + part)

        @pl.loop(0, seq // rows_m)
        def _(m):
            rows = pl.ds(pl.multiple_of(m * rows_m, rows_m), rows_m)
            x_s[rows, cols] = (x_s[rows, cols].astype(F32) + acc_s[rows, :]).astype(BF16)

        pltpu.make_async_copy(x_s.at[:, cols], y_ref.at[:, cols], io_sem.at[3]).start()

    def gather_norms():
        pltpu.make_async_copy(gln.at[:, :, :, :, pl.ds(0, 2 * LANES)], lnbuf, io_sem.at[4]).start()
        wait_on(lnbuf, io_sem.at[4])
        lnv[...] = jnp.zeros_like(lnv)
        share = cfg["share"]
        for dev in range(2 * side * side):
            start = dev * share // LANES * LANES
            width = min(2 * LANES, d_model - start)
            lnv[:, start:start + width] += lnbuf[dev // (2 * side), dev // 2 % side, dev % 2, :, :width]

    ln_rows = cfg["ln_rows"]

    def normalize(which):
        @pl.loop(0, seq // ln_rows)
        def _(m):
            rows = pl.ds(pl.multiple_of(m * ln_rows, ln_rows), ln_rows)
            acts = x_s[rows, :].astype(F32)
            centered = acts - jnp.mean(acts, axis=1, keepdims=True)
            variance = jnp.mean(centered * centered, axis=1, keepdims=True)
            gain, bias = lnv[which:which + 1, :], lnv[which + 1:which + 2, :]
            h_s[rows, :] = (centered * lax.rsqrt(variance + LN_EPS) * (1.0 + gain) + bias).astype(BF16)

    for blk in range(3):
        phase_1a(blk)
    pltpu.make_async_copy(x_ref, x_s, io_sem.at[0]).start()
    staged = []
    for idx, (name, r0, c0) in enumerate(cfg["staging"]):
        src = shards[name][0]
        spot = a_s.at[pl.ds(r0, src.shape[0]), pl.ds(c0, src.shape[1])]
        staged.append((shards[name][1], spot, src))
        pltpu.make_async_copy(src, spot, stage_sem.at[idx]).start()
    staged.append((gln, lnst, ln_ref))
    pltpu.make_async_copy(ln_ref, lnst, stage_sem.at[len(staged) - 1]).start()
    for idx, (g, spot, src) in enumerate(staged):
        wait_on(spot, stage_sem.at[idx])
        pltpu.make_async_copy(spot, g.at[y, x, c], own_sem.at[idx]).start()
    phase_1b(0)
    phase_1a(3)
    for idx, (g, spot, src) in enumerate(staged):
        wait_on(spot, own_sem.at[idx])
    phase_2a(0)
    phase_1b(1)
    phase_1a(4)
    phase_1b(2)

    kv_width, q_half, up_part = gk.shape[-1], gq.shape[-1] // 2, gu.shape[-1] // 6

    def first_norm():
        wait_on(x_s, io_sem.at[0])
        gather_norms()
        normalize(0)

    def k_part():
        kv_tiles(gk, k_s, True, kv_width)
        pltpu.make_async_copy(k_s, k_out, io_sem.at[1]).start()

    def v_part():
        kv_tiles(gv, v_s, False, kv_width)
        pltpu.make_async_copy(v_s, v_out, io_sem.at[2]).start()

    def up(i):
        return lambda: up_tiles(i * up_part, up_part)

    def down(i):
        return lambda: down_tile(i * tile)

    def blocks_in(*ids):
        def take():
            for blk in ids:
                ready(blk)
        return take

    half_kv = n_kv // 2
    plan = {
        2: ((blocks_in(0), first_norm), ()),
        3: ((blocks_in(1), k_part), ()),
        4: ((blocks_in(2), v_part), ()),
        5: ((blocks_in(3), lambda: q_tiles(0, q_half)), ()),
        6: ((blocks_in(4), lambda: q_tiles(q_half, q_half)), ()),
        7: ((lambda: attention(0, half_kv // 2),), (lambda: attention(half_kv // 2, half_kv),)),
        8: ((lambda: attention(half_kv, half_kv + half_kv // 2),), (lambda: attention(half_kv + half_kv // 2, n_kv),)),
        9: ((blocks_in(5, 6), lambda: o_tiles(0, q_half)), (lambda: o_tiles(q_half, q_half),)),
        10: ((lambda: normalize(2),), (blocks_in(7), up(0))),
        11: ((blocks_in(8), up(1)), (blocks_in(9), up(2))),
        12: ((blocks_in(10), up(3)), ()),
        13: ((blocks_in(11), up(4)), ()),
        14: ((blocks_in(12), up(5)), ()),
        15: ((blocks_in(13), down(0)), ()),
        16: ((blocks_in(14), down(1)), ()),
        17: ((blocks_in(15), down(2)), ()),
        18: ((blocks_in(16), down(3)), ()),
    }
    for j in range(n_blk):
        service(j)
        early, late = plan.get(j, ((), ()))
        for piece in early:
            piece()
        if j >= 1:
            finish(j - 1)
        for piece in late:
            piece()
    finish(n_blk - 1)
    ready(17)
    down_tile(4 * tile)
    ready(18)
    down_tile(5 * tile)
    wait_on(k_s, io_sem.at[1])
    wait_on(v_s, io_sem.at[2])
    wait_on(x_s, io_sem.at[3])
    for blk in range(n_blk):
        wait_send(blk)


def run_layer(n, x_loc, len_loc, cos_tab, sin_tab, ln_part, wq, wk, wv, wo, wu, wd, scale=1):
    seq, d_model = x_loc.shape
    side = math.isqrt(n // 2)
    tile = 512 // scale
    nq, nkv, ff = wq.shape[1], wk.shape[1], wu.shape[1]
    half = nq // 2
    blocks = [("ln", 0, ln_part.shape[1]), ("k", 0, nkv), ("v", 0, nkv), ("q", 0, half), ("q", half, half),
              ("o", 0, d_model // 2), ("o", d_model // 2, d_model // 2)]
    blocks += [("u", i * (ff // 6), ff // 6) for i in range(6)]
    blocks += [("d", i * (d_model // 6), d_model // 6) for i in range(6)]
    share = wq.shape[0]
    staging = [("q", 0, 0), ("k", 0, nq), ("v", 0, nq + nkv), ("o", 0, nq + 2 * nkv), ("u", share, 0), ("d", 2 * share, 0)]
    cfg = dict(side=side, tile=tile, rows_m=512 // scale, q_rows=256 // scale, ln_rows=64, share=share, blocks=blocks,
               staging=staging)
    vmem, hbm = pltpu.VMEM, pl.BlockSpec(memory_space=pltpu.HBM)

    def gathered(part):
        return jax.ShapeDtypeStruct((side, side, 2) + part.shape, part.dtype)

    flops = 2 * seq * (d_model * (nq + 2 * nkv + ff) + nq * d_model + ff * d_model)
    outs = pl.pallas_call(
        functools.partial(layer_kernel, cfg),
        out_shape=[jax.ShapeDtypeStruct((seq, d_model), BF16), jax.ShapeDtypeStruct((nkv // HEAD_DIM, seq, HEAD_DIM), BF16),
                   jax.ShapeDtypeStruct((nkv // HEAD_DIM, seq, HEAD_DIM), BF16)]
        + [gathered(part) for part in (ln_part, wq, wk, wv, wo, wu, wd)],
        in_specs=[pl.BlockSpec(memory_space=pltpu.SMEM), pl.BlockSpec(memory_space=vmem), pl.BlockSpec(memory_space=vmem)] + [hbm] * 8,
        out_specs=[hbm] * 10,
        scratch_shapes=[
            vmem((seq, d_model), BF16), vmem((seq, d_model), BF16), vmem((nq // HEAD_DIM, seq, HEAD_DIM), BF16),
            vmem((nkv // HEAD_DIM, seq, HEAD_DIM), BF16), vmem((nkv // HEAD_DIM, seq, HEAD_DIM), BF16), vmem((seq, ff), BF16),
            vmem((2, side, side, 2, share, tile), BF16), vmem((2, side, 2, wd.shape[0], tile), BF16), vmem((seq, tile), F32),
            vmem((ln_part.shape[0], d_model), F32), vmem((side, side, 2, ln_part.shape[0], 2 * LANES), F32), vmem(ln_part.shape, F32),
            pltpu.SemaphoreType.DMA((len(blocks), 5)), pltpu.SemaphoreType.DMA((len(blocks), 5)),
            pltpu.SemaphoreType.DMA((7,)), pltpu.SemaphoreType.DMA((7,)), pltpu.SemaphoreType.DMA((2,)),
            pltpu.SemaphoreType.DMA((2,)), pltpu.SemaphoreType.DMA((5,)),
        ],
        compiler_params=pltpu.CompilerParams(collective_id=0, has_side_effects=True, vmem_limit_bytes=67043328),
        cost_estimate=pl.CostEstimate(flops=flops, bytes_accessed=4 * n * wd.size, transcendentals=0),
    )(len_loc, cos_tab, sin_tab, x_loc, ln_part, wq, wk, wv, wo, wu, wd)
    return outs[:3]


def solution(mesh, scale=1):
    batch_spec = P(("rep", "wg"))
    row_spec = P("wg")
    n = mesh.shape["wg"]

    def local_layer(x_loc, lengths, positions, wq, wk, wv, wo, wu, wd, gain1, bias1, gain2, bias2):
        n_seq, seq, d_model = x_loc.shape
        cos_tab, sin_tab = rotary_tables(positions[0])
        share = gain1.shape[0]
        first_lane = lax.rem(lax.axis_index("wg") * share, LANES)
        stacked = jnp.stack([gain1, bias1, gain2, bias2])
        ln_part = lax.dynamic_update_slice(jnp.zeros((8, 4 * LANES), F32), stacked, (0, first_lane))
        y_out, k_heads, v_heads = run_layer(n, x_loc[0], lengths, cos_tab, sin_tab, ln_part, wq, wk, wv, wo, wu, wd, scale)
        return y_out[None], jnp.swapaxes(k_heads, 0, 1)[None], jnp.swapaxes(v_heads, 0, 1)[None]

    return jax.shard_map(local_layer, mesh=mesh, in_specs=(batch_spec, batch_spec, batch_spec) + (row_spec,) * 10,
                         out_specs=(batch_spec, batch_spec, batch_spec), check_vma=False)
```

time: 671 us -> 483 us (0.72)
  Pallas kernels: 0 us -> 456 us
  matrix products: 263 us -> 0 us
  waiting for transfers between devices: 194 us -> 0 us
  local copies, waits for them, and re-layouts: 88.9 us -> 12 us
  blocking collectives: 50.9 us -> 0 us
  other arithmetic: 53.8 us -> 4.63 us
  between operations: 15.9 us -> 1.77 us
    pallas_call x0 -> x1, Pallas kernels: none -> 456 us  [run_layer(): pl.pallas_call(functools.partial(layer_kernel, cfg), out_shape=[jax.Shape...]
    dot_general x22 -> x0, matrix products: 263 us -> none  [the longest x1 70 us: local_layer(): jnp.dot(sq_relu, gather_rows(wdown_part), preferred_element_type=jnp.floa...]
    all_gather x6 -> x0, waiting for transfers between devices: 190 us -> none  [gather_rows(): return lax.all_gather(part_arr, 'wg', axis=0, tiled=True)]
    unnamed x1 -> x0, blocking collectives: 50.9 us -> none
    dot_general x3 -> x0, local copies, waits for them, and re-layouts: 42.2 us -> none  [the longest x1 24.6 us: local_layer(): jnp.dot(h_norm, gather_rows(wq_part), preferred_element_type=jnp.float32)]
    concatenate x5 -> x1, local copies, waits for them, and re-layouts: 27.7 us -> 0.07 us  [rotary_tables(): jnp.concatenate([cos, cos, pad], axis=1)]
    reduce_sum x11 -> x0, other arithmetic: 26.7 us -> none  [the longest x8 19.3 us: causal_attention(): prob_bf = jax.nn.softmax(scores, axis=-1).astype(jnp.bfloat16)]
    concatenate x1, other arithmetic: 9.9 us -> 1.31 us  [rotary_tables(): jnp.concatenate([-sin, sin, pad], axis=1)]
  transfers between devices with their start and end apart: 6 -> 0, of which waited for: 4 -> 0; matrix products, arithmetic and copies ran while one was open for 49% -> 0% of each run, Pallas kernels for 0% -> 0%
where the time goes in v1:
time: 483 us; the launch traced here: 475 us
  Pallas kernels  456 us (94%)
  local copies, waits for them, and re-layouts  12 us (2%)
    pallas_call x1, Pallas kernels, run_layer(): pl.pallas_call(functools.partial(layer_kernel, cfg), out_shape=[jax.Shape...  456 us
    unnamed x7, local copies, waits for them, and re-layouts  11.4 us

profile of v1, /device:TPU:97, one launch (start us, length us, event | category | flops | bytes accessed | tf_op | source)
XLA Modules:
  0.0 474.5 jit_solution(17448088357114485714)
XLA Ops:
  1.3 0.1 pad.9.clone
  1.4 0.7 pad_maximum_fusion
  2.1 0.7 convert_element_type.10
  2.8 0.5 dynamic_update_slice.3.ln_ref
  3.3 0.0 copy-start.1
  3.3 1.9 fusion
  5.2 1.3 maximum_maximum_fusion.1
  6.5 0.0 copy-done.1
  6.5 456.2 %shard_map.148 = (bf16[1024,3072]{1,0:T(8,128)(2,1)}, bf16[8,1024,128]{2,1,0:T(8,128)(2,1)}, bf16[8,1024,128]{2,1,0:T(8,128)(2,1)}, f32[4,4,2,8,512]{4,3,2,1,0:T...) custom-call(s32[1]{0:T(128)S(6)} %copy.23.len_ref, ...), custom_call_target="tpu_custom_call" | custom-call | flops 167503724544 | bytes 113246208 | tf_op jit(solution)/shard_map/pallas_call | solution.py:413
  462.7 0.0 copy-start
  462.7 4.4 copy.19
  467.1 4.3 copy.20
  471.4 0.0 copy-done
  471.4 2.7 copy.24
  (3 shorter events, 0.0 us)
Async XLA Ops:
  3.3 3.2 copy-start.1
  462.7 8.7 %copy-start = (bf16[1024,3072]{1,0:T(8,128)(2,1)S(1)}, bf16[1024,3072]{1,0:T(8,128)(2,1)}, u32[]{:S(2)}) copy-start(bf16[1024,3072]{1,0:T(8,128)(2,1)} %get-tuple-element.6) | copy-start | bytes 18874372

commit v2 on v1

--- a/solution.py
+++ b/solution.py
@@ -20,15 +20,13 @@
 def rotary_tables(positions):
     quarter = HEAD_DIM // 4
     inv_freq = ROPE_BASE ** (-jnp.arange(quarter, dtype=F32) / quarter)
-    angles = positions.astype(F32)[:, None] * inv_freq
-    cos, sin = jnp.cos(angles), jnp.sin(angles)
-    pad = jnp.zeros((positions.shape[0], 2 * quarter), F32)
-    return jnp.concatenate([cos, cos, pad], axis=1), jnp.concatenate([-sin, sin, pad], axis=1)
+    angles = positions.astype(F32)[None, :] * inv_freq[:, None]
+    return jnp.cos(angles), jnp.sin(angles)
 
 
 def layer_kernel(cfg, len_ref, cos_ref, sin_ref, x_ref, ln_ref, wq_ref, wk_ref, wv_ref, wo_ref, wu_ref, wd_ref,
                  y_ref, k_out, v_out, gln, gq, gk, gv, go, gu, gd,
-                 x_s, h_s, q_s, k_s, v_s, a_s, wb, wbd, acc_s, lnv, lnbuf, lnst,
+                 x_s, h_s, q_s, k_s, v_s, a_s, wb, wbd, acc_s, cos_s, sin_s, turn_s, lnv, lnbuf, lnst,
                  send_sem, recv_sem, stage_sem, own_sem, wb_sem, wbd_sem, io_sem):
     side = cfg["side"]
     seq, d_model = x_s.shape
@@ -67,9 +65,17 @@
 
     def cols_of(blk):
         name, c0, width = blocks[blk]
-        half, quarter = width // 2, width // 4
-        return (pl.ds(c0, half), pl.ds(c0, quarter), pl.ds(c0 + quarter, quarter),
-                pl.ds(c0 + half, half), pl.ds(c0 + half, quarter), pl.ds(c0 + half + quarter, quarter), pl.ds(c0, width))
+        half = width // 2
+        return pl.ds(c0, half), pl.ds(c0 + half, half), pl.ds(c0, width)
+
+    def parts_of(blk):
+        name, c0, width = blocks[blk]
+        half, quarter, depth = width // 2, width // 4, shards[name][0].shape[0]
+        if quarter < cfg["lanes"]:
+            rows = (pl.ds(0, depth // 2), pl.ds(depth // 2, depth // 2))
+            return [(r, pl.ds(start, half)) for start in (c0, c0 + half) for r in rows]
+        every = pl.ds(0, depth)
+        return [(every, pl.ds(c0 + i * quarter, quarter)) for i in range(4)]
 
     def unit_refs(blk):
         name, c0, width = blocks[blk]
@@ -90,7 +96,7 @@
 
     def phase_1a(blk):
         w, g = shards[blocks[blk][0]]
-        ca, _, _, cb, _, _, cw = cols_of(blk)
+        ca, cb, cw = cols_of(blk)
         put(blk, 0, w.at[:, ca], g.at[y, x, c, :, ca], d_xp)
         put(blk, 0, w.at[:, ca], g.at[y, x, c, :, ca], d_xm)
         put(blk, 0, w.at[:, cb], g.at[y, x, c, :, cb], d_yp)
@@ -99,12 +105,13 @@
 
     def phase_1b(blk):
         g = shards[blocks[blk][0]][1]
-        ca, a0, a1, cb, b0, b1, _ = cols_of(blk)
+        ca, cb, _ = cols_of(blk)
+        a0, a1, b0, b1 = parts_of(blk)
         wait_recv(blk, 0)
-        same(blk, 1, g.at[y, xm, c, :, a0], d_xp)
-        same(blk, 1, g.at[y, xp, c, :, a1], d_xm)
-        same(blk, 1, g.at[ym, x, c, :, b0], d_yp)
-        same(blk, 1, g.at[yp, x, c, :, b1], d_ym)
+        same(blk, 1, g.at[(y, xm, c) + a0], d_xp)
+        same(blk, 1, g.at[(y, xp, c) + a1], d_xm)
+        same(blk, 1, g.at[(ym, x, c) + b0], d_yp)
+        same(blk, 1, g.at[(yp, x, c) + b1], d_ym)
         same(blk, 4, g.at[y, xm, c, :, ca], d_peer)
         same(blk, 4, g.at[y, xp, c, :, ca], d_peer)
         same(blk, 4, g.at[ym, x, c, :, cb], d_peer)
@@ -112,7 +119,7 @@
 
     def phase_2a(blk):
         g = shards[blocks[blk][0]][1]
-        ca, _, _, cb, _, _, _ = cols_of(blk)
+        ca, cb, _ = cols_of(blk)
         wait_recv(blk, 1)
         same(blk, 2, g.at[y, :, c, :, ca], d_yp)
         same(blk, 2, g.at[y, :, c, :, ca], d_ym)
@@ -123,11 +130,13 @@
 
     def phase_2b(blk):
         g = shards[blocks[blk][0]][1]
-        ca, a0, a1, cb, b0, b1, _ = cols_of(blk)
-        same(blk, 3, g.at[ym, :, c, :, a0], d_yp)
-        same(blk, 3, g.at[yp, :, c, :, a1], d_ym)
-        same(blk, 3, g.at[:, xm, c, :, b0], d_xp)
-        same(blk, 3, g.at[:, xp, c, :, b1], d_xm)
+        ca, cb, _ = cols_of(blk)
+        a0, a1, b0, b1 = parts_of(blk)
+        every = pl.ds(0, side)
+        same(blk, 3, g.at[(ym, every, c) + a0], d_yp)
+        same(blk, 3, g.at[(yp, every, c) + a1], d_ym)
+        same(blk, 3, g.at[(every, xm, c) + b0], d_xp)
+        same(blk, 3, g.at[(every, xp, c) + b1], d_xm)
         same(blk, 4, g.at[ym, :, c, :, ca], d_peer)
         same(blk, 4, g.at[yp, :, c, :, ca], d_peer)
         same(blk, 4, g.at[:, xm, c, :, cb], d_peer)
@@ -135,7 +144,7 @@
 
     def finish(blk):
         g = shards[blocks[blk][0]][1]
-        ca, _, _, cb, _, _, _ = cols_of(blk)
+        ca, cb, _ = cols_of(blk)
         wait_recv(blk, 3)
         same(blk, 4, g.at[yo, :, c, :, ca], d_peer)
         same(blk, 4, g.at[:, xo, c, :, cb], d_peer)
@@ -147,9 +156,11 @@
 
     def service(j):
         wait_recv(j, 2)
-        if j + 1 < n_blk:
+        if j + 1 < n_blk - 1:
             phase_2a(j + 1)
         phase_2b(j)
+        if j == n_blk - 3:
+            phase_2a(n_blk - 1)
         if j + 3 < n_blk:
             phase_1b(j + 3)
         if j + 5 < n_blk:
@@ -183,7 +194,7 @@
 
     def rotate(vals, rows):
         swapped = jnp.where(lane < eighth, pltpu.roll(vals, HEAD_DIM - eighth, 1), pltpu.roll(vals, eighth, 1))
-        turned = vals * cos_ref[rows, :] + swapped * sin_ref[rows, :]
+        turned = vals * cos_s[rows, :] + swapped * sin_s[rows, :]
         return jnp.where(lane < 2 * eighth, turned, vals)
 
     heads_per_tile = tile // HEAD_DIM
@@ -244,38 +255,63 @@
 
         matmul_tiles(gu, col0, width // tile, epilogue)
 
-    def down_tile(col0):
-        cols = pl.ds(col0, tile)
+    def down_pieces(first, count):
+        width = tile // 2
         depth = a_s.shape[1] // side
 
-        def fetch(k, slot):
-            return pltpu.make_async_copy(gd.at[k, :, :, :, cols], wbd.at[slot], wbd_sem.at[slot])
-
-        fetch(0, 0).start()
-
-        @pl.loop(0, side)
-        def _(k):
-            slot = lax.rem(k, 2)
-
-            @pl.when(k + 1 < side)
-            def _():
-                fetch(k + 1, lax.rem(k + 1, 2)).start()
-
-            fetch(k, slot).wait()
-            deep = pl.ds(pl.multiple_of(k * depth, LANES), depth)
+        @pl.loop(0, count)
+        def _(piece):
+            cols = pl.ds(pl.multiple_of((first + piece) * width, LANES), width)
+
+            def fetch(k, slot):
+                return pltpu.make_async_copy(gd.at[k, :, :, :, cols], wbd.at[slot], wbd_sem.at[slot])
+
+            fetch(0, 0).start()
+
+            @pl.loop(0, side)
+            def _(k):
+                slot = lax.rem(k, 2)
+
+                @pl.when(k + 1 < side)
+                def _():
+                    fetch(k + 1, lax.rem(k + 1, 2)).start()
+
+                fetch(k, slot).wait()
+                deep = pl.ds(pl.multiple_of(k * depth, LANES), depth)
+
+                @pl.loop(0, seq // rows_m)
+                def _(m):
+                    rows = pl.ds(pl.multiple_of(m * rows_m, rows_m), rows_m)
+                    part = jnp.dot(a_s[rows, deep], wbd[slot].reshape(depth, width), preferred_element_type=F32)
+                    acc_s[rows, :] = jnp.where(k == 0, part, acc_s[rows, :] + part)
 
             @pl.loop(0, seq // rows_m)
             def _(m):
                 rows = pl.ds(pl.multiple_of(m * rows_m, rows_m), rows_m)
-                part = jnp.dot(a_s[rows, deep], wbd[slot].reshape(depth, tile), preferred_element_type=F32)
-                acc_s[rows, :] = jnp.where(k == 0, part, acc_s[rows, :] + part)
-
-        @pl.loop(0, seq // rows_m)
+                x_s[rows, cols] = (x_s[rows, cols].astype(F32) + acc_s[rows, :]).astype(BF16)
+
+            pltpu.make_async_copy(x_s.at[:, cols], y_ref.at[:, cols], io_sem.at[3]).start()
+
+    def make_tables():
+        span = cfg["span"]
+
+        @pl.loop(0, seq // span)
         def _(m):
-            rows = pl.ds(pl.multiple_of(m * rows_m, rows_m), rows_m)
-            x_s[rows, cols] = (x_s[rows, cols].astype(F32) + acc_s[rows, :]).astype(BF16)
-
-        pltpu.make_async_copy(x_s.at[:, cols], y_ref.at[:, cols], io_sem.at[3]).start()
+            rows = pl.ds(pl.multiple_of(m * span, span), span)
+            cos, sin = cos_ref[:, rows].T, sin_ref[:, rows].T
+            pad = jnp.zeros((span, 2 * eighth), F32)
+            cos_s[rows, :] = jnp.concatenate([cos, cos, pad], axis=1)
+            sin_s[rows, :] = jnp.concatenate([-sin, sin, pad], axis=1)
+
+    def heads_inward(src, out, sem):
+        step = 64
+
+        @pl.loop(0, seq // step)
+        def _(m):
+            rows = pl.ds(pl.multiple_of(m * step, step), step)
+            turn_s[rows, :, :] = jnp.swapaxes(src[:, rows, :].astype(F32), 0, 1).astype(BF16)
+
+        pltpu.make_async_copy(turn_s, out, sem).start()
 
     def gather_norms():
         pltpu.make_async_copy(gln.at[:, :, :, :, pl.ds(0, 2 * LANES)], lnbuf, io_sem.at[4]).start()
@@ -329,62 +365,83 @@
         gather_norms()
         normalize(0)
 
-    def k_part():
-        kv_tiles(gk, k_s, True, kv_width)
-        pltpu.make_async_copy(k_s, k_out, io_sem.at[1]).start()
-
-    def v_part():
-        kv_tiles(gv, v_s, False, kv_width)
-        pltpu.make_async_copy(v_s, v_out, io_sem.at[2]).start()
-
-    def up(i):
-        return lambda: up_tiles(i * up_part, up_part)
-
-    def down(i):
-        return lambda: down_tile(i * tile)
-
-    def blocks_in(*ids):
-        def take():
-            for blk in ids:
-                ready(blk)
-        return take
+    def caches():
+        heads_inward(k_s, k_out, io_sem.at[1])
+        wait_on(turn_s, io_sem.at[1])
+        heads_inward(v_s, v_out, io_sem.at[2])
+        wait_on(turn_s, io_sem.at[2])
 
     half_kv = n_kv // 2
-    plan = {
-        2: ((blocks_in(0), first_norm), ()),
-        3: ((blocks_in(1), k_part), ()),
-        4: ((blocks_in(2), v_part), ()),
-        5: ((blocks_in(3), lambda: q_tiles(0, q_half)), ()),
-        6: ((blocks_in(4), lambda: q_tiles(q_half, q_half)), ()),
-        7: ((lambda: attention(0, half_kv // 2),), (lambda: attention(half_kv // 2, half_kv),)),
-        8: ((lambda: attention(half_kv, half_kv + half_kv // 2),), (lambda: attention(half_kv + half_kv // 2, n_kv),)),
-        9: ((blocks_in(5, 6), lambda: o_tiles(0, q_half)), (lambda: o_tiles(q_half, q_half),)),
-        10: ((lambda: normalize(2),), (blocks_in(7), up(0))),
-        11: ((blocks_in(8), up(1)), (blocks_in(9), up(2))),
-        12: ((blocks_in(10), up(3)), ()),
-        13: ((blocks_in(11), up(4)), ()),
-        14: ((blocks_in(12), up(5)), ()),
-        15: ((blocks_in(13), down(0)), ()),
-        16: ((blocks_in(14), down(1)), ()),
-        17: ((blocks_in(15), down(2)), ()),
-        18: ((blocks_in(16), down(3)), ()),
-    }
-    for j in range(n_blk):
+
+    def stage(j):
         service(j)
-        early, late = plan.get(j, ((), ()))
-        for piece in early:
-            piece()
+        if j == 2:
+            ready(0)
+            first_norm()
+            make_tables()
+        if j == 3:
+            ready(1)
+            kv_tiles(gk, k_s, True, kv_width)
+        if j == 4:
+            ready(2)
+            kv_tiles(gv, v_s, False, kv_width)
+        if j == 5:
+            caches()
+        if j == 6:
+            ready(3)
+            ready(4)
+            q_tiles(0, 2 * q_half)
+        if j == 7:
+            attention(0, half_kv)
+        if j == 8:
+            attention(half_kv, n_kv)
+        if j == 9:
+            ready(5)
+            ready(6)
+            o_tiles(0, d_model)
+        if j == 10:
+            normalize(2)
+            ready(7)
+            ready(8)
+            up_tiles(0, 2 * up_part)
+        if j == 12:
+            ready(9)
+            ready(10)
+            up_tiles(2 * up_part, 2 * up_part)
+        if j == 14:
+            ready(11)
+            ready(12)
+            up_tiles(4 * up_part, 2 * up_part)
+        if j == 15:
+            ready(13)
+            down_pieces(0, 2)
+        if j == 16:
+            ready(14)
+            down_pieces(2, 2)
+        if j == 18:
+            down_pieces(7, 1)
+        if j == 19:
+            down_pieces(9, 1)
         if j >= 1:
             finish(j - 1)
-        for piece in late:
-            piece()
-    finish(n_blk - 1)
-    ready(17)
-    down_tile(4 * tile)
-    ready(18)
-    down_tile(5 * tile)
-    wait_on(k_s, io_sem.at[1])
-    wait_on(v_s, io_sem.at[2])
+        if j == 16:
+            ready(15)
+            down_pieces(4, 2)
+        if j == 17:
+            ready(16)
+            down_pieces(6, 1)
+        if j == 18:
+            ready(17)
+            down_pieces(8, 1)
+        if j == 19:
+            finish(19)
+            ready(18)
+            down_pieces(10, 1)
+            ready(19)
+            down_pieces(11, 1)
+
+    for j in range(n_blk):
+        stage(j)
     wait_on(x_s, io_sem.at[3])
     for blk in range(n_blk):
         wait_send(blk)
@@ -399,11 +456,11 @@
     blocks = [("ln", 0, ln_part.shape[1]), ("k", 0, nkv), ("v", 0, nkv), ("q", 0, half), ("q", half, half),
               ("o", 0, d_model // 2), ("o", d_model // 2, d_model // 2)]
     blocks += [("u", i * (ff // 6), ff // 6) for i in range(6)]
-    blocks += [("d", i * (d_model // 6), d_model // 6) for i in range(6)]
+    blocks += [("d", i * tile, tile) for i in range(5)] + [("d", 5 * tile, tile // 2), ("d", 11 * tile // 2, tile // 2)]
     share = wq.shape[0]
     staging = [("q", 0, 0), ("k", 0, nq), ("v", 0, nq + nkv), ("o", 0, nq + 2 * nkv), ("u", share, 0), ("d", 2 * share, 0)]
     cfg = dict(side=side, tile=tile, rows_m=512 // scale, q_rows=256 // scale, ln_rows=64, share=share, blocks=blocks,
-               staging=staging)
+               staging=staging, lanes=LANES // scale, span=LANES)
     vmem, hbm = pltpu.VMEM, pl.BlockSpec(memory_space=pltpu.HBM)
 
     def gathered(part):
@@ -412,15 +469,16 @@
     flops = 2 * seq * (d_model * (nq + 2 * nkv + ff) + nq * d_model + ff * d_model)
     outs = pl.pallas_call(
         functools.partial(layer_kernel, cfg),
-        out_shape=[jax.ShapeDtypeStruct((seq, d_model), BF16), jax.ShapeDtypeStruct((nkv // HEAD_DIM, seq, HEAD_DIM), BF16),
-                   jax.ShapeDtypeStruct((nkv // HEAD_DIM, seq, HEAD_DIM), BF16)]
+        out_shape=[jax.ShapeDtypeStruct((seq, d_model), BF16), jax.ShapeDtypeStruct((seq, nkv // HEAD_DIM, HEAD_DIM), BF16),
+                   jax.ShapeDtypeStruct((seq, nkv // HEAD_DIM, HEAD_DIM), BF16)]
         + [gathered(part) for part in (ln_part, wq, wk, wv, wo, wu, wd)],
         in_specs=[pl.BlockSpec(memory_space=pltpu.SMEM), pl.BlockSpec(memory_space=vmem), pl.BlockSpec(memory_space=vmem)] + [hbm] * 8,
         out_specs=[hbm] * 10,
         scratch_shapes=[
             vmem((seq, d_model), BF16), vmem((seq, d_model), BF16), vmem((nq // HEAD_DIM, seq, HEAD_DIM), BF16),
             vmem((nkv // HEAD_DIM, seq, HEAD_DIM), BF16), vmem((nkv // HEAD_DIM, seq, HEAD_DIM), BF16), vmem((seq, ff), BF16),
-            vmem((2, side, side, 2, share, tile), BF16), vmem((2, side, 2, wd.shape[0], tile), BF16), vmem((seq, tile), F32),
+            vmem((2, side, side, 2, share, tile), BF16), vmem((2, side, 2, wd.shape[0], tile // 2), BF16), vmem((seq, tile // 2), F32),
+            vmem((seq, HEAD_DIM), F32), vmem((seq, HEAD_DIM), F32), vmem((seq, nkv // HEAD_DIM, HEAD_DIM), BF16),
             vmem((ln_part.shape[0], d_model), F32), vmem((side, side, 2, ln_part.shape[0], 2 * LANES), F32), vmem(ln_part.shape, F32),
             pltpu.SemaphoreType.DMA((len(blocks), 5)), pltpu.SemaphoreType.DMA((len(blocks), 5)),
             pltpu.SemaphoreType.DMA((7,)), pltpu.SemaphoreType.DMA((7,)), pltpu.SemaphoreType.DMA((2,)),
@@ -444,8 +502,8 @@
         first_lane = lax.rem(lax.axis_index("wg") * share, LANES)
         stacked = jnp.stack([gain1, bias1, gain2, bias2])
         ln_part = lax.dynamic_update_slice(jnp.zeros((8, 4 * LANES), F32), stacked, (0, first_lane))
-        y_out, k_heads, v_heads = run_layer(n, x_loc[0], lengths, cos_tab, sin_tab, ln_part, wq, wk, wv, wo, wu, wd, scale)
-        return y_out[None], jnp.swapaxes(k_heads, 0, 1)[None], jnp.swapaxes(v_heads, 0, 1)[None]
+        y_out, k_cache, v_cache = run_layer(n, x_loc[0], lengths, cos_tab, sin_tab, ln_part, wq, wk, wv, wo, wu, wd, scale)
+        return y_out[None], k_cache[None], v_cache[None]
 
     return jax.shard_map(local_layer, mesh=mesh, in_specs=(batch_spec, batch_spec, batch_spec) + (row_spec,) * 10,
                          out_specs=(batch_spec, batch_spec, batch_spec), check_vma=False)

time: 483 us -> 485 us (level); the launches traced: 475 us -> 484 us
  Pallas kernels: 456 us -> 471 us
    pallas_call x1, Pallas kernels: 456 us -> 471 us  [run_layer(): pl.pallas_call(functools.partial(layer_kernel, cfg), out_shape=[jax.Shape...]
    unnamed x7 -> x9, local copies, waits for them, and re-layouts: 11.4 us -> 8.76 us
where the time goes in v2:
time: 485 us; the launch traced here: 484 us
  Pallas kernels  471 us (97%)
  local copies, waits for them, and re-layouts  9.27 us (2%)
    pallas_call x1, Pallas kernels, run_layer(): pl.pallas_call(functools.partial(layer_kernel, cfg), out_shape=[jax.Shape...  471 us

profile of v2, /device:TPU:97, one launch (start us, length us, event | category | flops | bytes accessed | tf_op | source)
XLA Modules:
  0.0 484.4 jit_solution(9752107432755648682)
XLA Ops:
  1.3 0.7 pad_maximum_fusion
  2.0 0.7 convert_element_type.4
  2.7 0.5 dynamic_update_slice.3.ln_ref
  3.2 0.0 copy-start.2
  3.2 1.3 multiply_sine_fusion
  4.5 0.0 copy-done.2
  4.5 471.1 %shard_map.148 = (bf16[1024,3072]{1,0:T(8,128)(2,1)}, bf16[1024,8,128]{2,1,0:T(8,128)(2,1)}, bf16[1024,8,128]{2,1,0:T(8,128)(2,1)}, f32[4,4,2,8,512]{4,3,2,1,0:T...) custom-call(s32[1]{0:T(128)S(6)} %copy.20.len_ref, ...), custom_call_target="tpu_custom_call" | custom-call | flops 167503724544 | bytes 113246208 | tf_op jit(solution)/shard_map/pallas_call | solution.py:470
  475.6 0.0 copy-start.1
  475.6 0.0 copy-start
  475.6 6.1 %copy.21 = bf16[1,1024,3072]{2,1,0:T(8,128)(2,1)} copy(bf16[1,1024,3072]{2,1,0:T(8,128)(2,1)} %bitcast.9) | data formatting | bytes 12582912
  481.8 0.0 copy-done.1
  481.8 1.3 copy.22
  483.1 0.0 copy-done
  483.1 1.3 copy.23
  (2 shorter events, 0.0 us)
Async XLA Ops:
  3.2 1.3 copy-start.2
  475.6 6.1 %copy-start.1 = (bf16[1024,8,128]{2,1,0:T(8,128)(2,1)S(1)}, bf16[1024,8,128]{2,1,0:T(8,128)(2,1)}, u32[]{:S(2)}) copy-start(bf16[1024,8,128]{2,1,0:T(8,128)(2,1)} %get-tuple-element.7) | copy-start | bytes 6291460
  475.6 7.4 %copy-start = (bf16[1024,8,128]{2,1,0:T(8,128)(2,1)S(1)}, bf16[1024,8,128]{2,1,0:T(8,128)(2,1)}, u32[]{:S(2)}) copy-start(bf16[1024,8,128]{2,1,0:T(8,128)(2,1)} %get-tuple-element.8) | copy-start | bytes 6291460

commit v3 on v2

--- a/solution.py
+++ b/solution.py
@@ -156,20 +156,18 @@
 
     def service(j):
         wait_recv(j, 2)
-        if j + 1 < n_blk - 1:
-            phase_2a(j + 1)
+        if j + 4 < n_blk:
+            phase_1b(j + 4)
+        if j + 6 < n_blk:
+            phase_1a(j + 6)
         phase_2b(j)
-        if j == n_blk - 3:
-            phase_2a(n_blk - 1)
-        if j + 3 < n_blk:
-            phase_1b(j + 3)
-        if j + 5 < n_blk:
-            phase_1a(j + 5)
-
-    def matmul_tiles(g, col0, n_tiles, epilogue):
+        if j + 2 < n_blk:
+            phase_2a(j + 2)
+
+    def matmul_tiles(g, first, n_tiles, epilogue):
         def fetch(t, slot):
             return pltpu.make_async_copy(
-                g.at[:, :, :, :, pl.ds(pl.multiple_of(col0 + t * tile, LANES), tile)], wb.at[slot], wb_sem.at[slot])
+                g.at[:, :, :, :, pl.ds(pl.multiple_of((first + t) * tile, LANES), tile)], wb.at[slot], wb_sem.at[slot])
 
         fetch(0, 0).start()
 
@@ -187,7 +185,7 @@
             def _(m):
                 rows = pl.ds(pl.multiple_of(m * rows_m, rows_m), rows_m)
                 weights = wb[slot].reshape(d_model, tile)
-                epilogue(t, rows, m, jnp.dot(h_s[rows, :], weights, preferred_element_type=F32))
+                epilogue(first + t, rows, m, jnp.dot(h_s[rows, :], weights, preferred_element_type=F32))
 
     lane = lax.broadcasted_iota(jnp.int32, (rows_m, HEAD_DIM), 1)
     eighth = HEAD_DIM // 4
@@ -200,13 +198,13 @@
     heads_per_tile = tile // HEAD_DIM
     length = len_ref[0]
 
-    def q_tiles(col0, width):
+    def q_tiles(first, count):
         def epilogue(t, rows, m, acc):
             for i in range(heads_per_tile):
                 part = acc[:, i * HEAD_DIM:(i + 1) * HEAD_DIM]
-                q_s[col0 // HEAD_DIM + t * heads_per_tile + i, rows, :] = rotate(part, rows).astype(BF16)
-
-        matmul_tiles(gq, col0, width // tile, epilogue)
+                q_s[t * heads_per_tile + i, rows, :] = rotate(part, rows).astype(BF16)
+
+        matmul_tiles(gq, first, count, epilogue)
 
     def kv_tiles(g, out, turn, width):
         def epilogue(t, rows, m, acc):
@@ -223,74 +221,71 @@
     q_rows = cfg["q_rows"]
     score_scale = HEAD_DIM ** -0.5
 
-    def attention(g_lo, g_hi):
-        @pl.loop(g_lo, g_hi)
-        def _(kv):
+    def attention(head_lo, head_hi):
+        @pl.loop(head_lo, head_hi)
+        def _(head):
+            kv = head // per_kv
             for blk in range(seq // q_rows):
                 lo, hi = blk * q_rows, (blk + 1) * q_rows
                 key = lax.broadcasted_iota(jnp.int32, (q_rows, hi), 1)
                 query = lo + lax.broadcasted_iota(jnp.int32, (q_rows, hi), 0)
                 allowed = (key <= query) & (key < length)
-                for i in range(per_kv):
-                    head = kv * per_kv + i
-                    scores = lax.dot_general(q_s[head, lo:hi, :], k_s[kv, :hi, :], (((1,), (1,)), ((), ())),
-                                             preferred_element_type=F32) * score_scale
-                    scores = jnp.where(allowed, scores, -1e30)
-                    probs = jnp.exp(scores - jnp.max(scores, axis=1, keepdims=True))
-                    probs = probs * (1.0 / jnp.sum(probs, axis=1, keepdims=True))
-                    out = jnp.dot(probs.astype(BF16), v_s[kv, :hi, :], preferred_element_type=F32)
-                    h_s[lo:hi, pl.ds(pl.multiple_of(head * HEAD_DIM, HEAD_DIM), HEAD_DIM)] = out.astype(BF16)
-
-    def o_tiles(col0, width):
+                scores = lax.dot_general(q_s[head, lo:hi, :], k_s[kv, :hi, :], (((1,), (1,)), ((), ())),
+                                         preferred_element_type=F32) * score_scale
+                scores = jnp.where(allowed, scores, -1e30)
+                probs = jnp.exp(scores - jnp.max(scores, axis=1, keepdims=True))
+                probs = probs * (1.0 / jnp.sum(probs, axis=1, keepdims=True))
+                out = jnp.dot(probs.astype(BF16), v_s[kv, :hi, :], preferred_element_type=F32)
+                h_s[lo:hi, pl.ds(pl.multiple_of(head * HEAD_DIM, HEAD_DIM), HEAD_DIM)] = out.astype(BF16)
+
+    def o_tiles(first, count):
         def epilogue(t, rows, m, acc):
-            cols = pl.ds(pl.multiple_of(col0 + t * tile, LANES), tile)
+            cols = pl.ds(pl.multiple_of(t * tile, LANES), tile)
             x_s[rows, cols] = (x_s[rows, cols].astype(F32) + acc).astype(BF16)
 
-        matmul_tiles(go, col0, width // tile, epilogue)
-
-    def up_tiles(col0, width):
+        matmul_tiles(go, first, count, epilogue)
+
+    def up_tiles(first, count):
         def epilogue(t, rows, m, acc):
-            cols = pl.ds(pl.multiple_of(col0 + t * tile, LANES), tile)
+            cols = pl.ds(pl.multiple_of(t * tile, LANES), tile)
             a_s[rows, cols] = jnp.square(jnp.maximum(acc, 0.0)).astype(BF16)
 
-        matmul_tiles(gu, col0, width // tile, epilogue)
-
-    def down_pieces(first, count):
-        width = tile // 2
+        matmul_tiles(gu, first, count, epilogue)
+
+    def down(col0, width, m_lo=0, m_hi=seq // rows_m):
+        cols, wide = pl.ds(col0, width), pl.ds(0, width)
         depth = a_s.shape[1] // side
 
-        @pl.loop(0, count)
-        def _(piece):
-            cols = pl.ds(pl.multiple_of((first + piece) * width, LANES), width)
-
-            def fetch(k, slot):
-                return pltpu.make_async_copy(gd.at[k, :, :, :, cols], wbd.at[slot], wbd_sem.at[slot])
-
-            fetch(0, 0).start()
-
-            @pl.loop(0, side)
-            def _(k):
-                slot = lax.rem(k, 2)
-
-                @pl.when(k + 1 < side)
-                def _():
-                    fetch(k + 1, lax.rem(k + 1, 2)).start()
-
-                fetch(k, slot).wait()
-                deep = pl.ds(pl.multiple_of(k * depth, LANES), depth)
-
-                @pl.loop(0, seq // rows_m)
-                def _(m):
-                    rows = pl.ds(pl.multiple_of(m * rows_m, rows_m), rows_m)
-                    part = jnp.dot(a_s[rows, deep], wbd[slot].reshape(depth, width), preferred_element_type=F32)
-                    acc_s[rows, :] = jnp.where(k == 0, part, acc_s[rows, :] + part)
-
-            @pl.loop(0, seq // rows_m)
+        def fetch(k, slot):
+            return pltpu.make_async_copy(gd.at[k, :, :, :, cols], wbd.at[slot, :, :, :, wide], wbd_sem.at[slot])
+
+        fetch(0, 0).start()
+
+        @pl.loop(0, side)
+        def _(k):
+            slot = lax.rem(k, 2)
+
+            @pl.when(k + 1 < side)
+            def _():
+                fetch(k + 1, lax.rem(k + 1, 2)).start()
+
+            fetch(k, slot).wait()
+            deep = pl.ds(pl.multiple_of(k * depth, LANES), depth)
+
+            @pl.loop(m_lo, m_hi)
             def _(m):
                 rows = pl.ds(pl.multiple_of(m * rows_m, rows_m), rows_m)
-                x_s[rows, cols] = (x_s[rows, cols].astype(F32) + acc_s[rows, :]).astype(BF16)
-
-            pltpu.make_async_copy(x_s.at[:, cols], y_ref.at[:, cols], io_sem.at[3]).start()
+                weights = wbd[slot, :, :, :, wide].reshape(depth, width)
+                part = jnp.dot(a_s[rows, deep], weights, preferred_element_type=F32)
+                acc_s[rows, wide] = jnp.where(k == 0, part, acc_s[rows, wide] + part)
+
+        @pl.loop(m_lo, m_hi)
+        def _(m):
+            rows = pl.ds(pl.multiple_of(m * rows_m, rows_m), rows_m)
+            x_s[rows, cols] = (x_s[rows, cols].astype(F32) + acc_s[rows, wide]).astype(BF16)
+
+        span = pl.ds(m_lo * rows_m, (m_hi - m_lo) * rows_m)
+        pltpu.make_async_copy(x_s.at[span, cols], y_ref.at[span, cols], io_sem.at[3]).start()
 
     def make_tables():
         span = cfg["span"]
@@ -351,14 +346,17 @@
         pltpu.make_async_copy(spot, g.at[y, x, c], own_sem.at[idx]).start()
     phase_1b(0)
     phase_1a(3)
+    phase_1a(4)
     for idx, (g, spot, src) in enumerate(staged):
         wait_on(spot, own_sem.at[idx])
     phase_2a(0)
     phase_1b(1)
-    phase_1a(4)
+    phase_1a(5)
     phase_1b(2)
-
-    kv_width, q_half, up_part = gk.shape[-1], gq.shape[-1] // 2, gu.shape[-1] // 6
+    phase_2a(1)
+    phase_1b(3)
+
+    kv_width, halves = gk.shape[-1], seq // rows_m
 
     def first_norm():
         wait_on(x_s, io_sem.at[0])
@@ -371,7 +369,11 @@
         heads_inward(v_s, v_out, io_sem.at[2])
         wait_on(turn_s, io_sem.at[2])
 
-    half_kv = n_kv // 2
+    def arrive(*ids):
+        for blk in ids:
+            ready(blk)
+
+    eighth_heads = n_heads // 8
 
     def stage(j):
         service(j)
@@ -379,66 +381,86 @@
             ready(0)
             first_norm()
             make_tables()
-        if j == 3:
+            finish(1)
             ready(1)
             kv_tiles(gk, k_s, True, kv_width)
-        if j == 4:
+        elif j == 3:
+            finish(2)
             ready(2)
             kv_tiles(gv, v_s, False, kv_width)
-        if j == 5:
+        elif j == 4:
+            finish(3)
+            ready(3)
+            q_tiles(0, 3)
+        elif j == 5:
             caches()
-        if j == 6:
-            ready(3)
+            finish(4)
             ready(4)
-            q_tiles(0, 2 * q_half)
-        if j == 7:
-            attention(0, half_kv)
-        if j == 8:
-            attention(half_kv, n_kv)
-        if j == 9:
-            ready(5)
-            ready(6)
-            o_tiles(0, d_model)
-        if j == 10:
+            q_tiles(3, 3)
+        elif j == 6:
+            attention(0, 3 * eighth_heads)
+            finish(5)
+        elif j == 7:
+            attention(3 * eighth_heads, 6 * eighth_heads)
+            finish(6)
+        elif j == 8:
+            attention(6 * eighth_heads, n_heads)
+            finish(7)
+            arrive(5, 6)
+            o_tiles(0, 2)
+        elif j == 9:
+            o_tiles(2, 4)
+            finish(8)
             normalize(2)
-            ready(7)
-            ready(8)
-            up_tiles(0, 2 * up_part)
-        if j == 12:
-            ready(9)
-            ready(10)
-            up_tiles(2 * up_part, 2 * up_part)
-        if j == 14:
-            ready(11)
-            ready(12)
-            up_tiles(4 * up_part, 2 * up_part)
-        if j == 15:
-            ready(13)
-            down_pieces(0, 2)
-        if j == 16:
-            ready(14)
-            down_pieces(2, 2)
-        if j == 18:
-            down_pieces(7, 1)
-        if j == 19:
-            down_pieces(9, 1)
-        if j >= 1:
-            finish(j - 1)
-        if j == 16:
+        elif j == 10:
+            arrive(7, 8)
+            up_tiles(0, 5)
+            finish(9)
+        elif j == 11:
+            arrive(9)
+            up_tiles(5, 4)
+            finish(10)
+        elif j == 12:
+            arrive(10)
+            up_tiles(9, 3)
+            finish(11)
+        elif j == 13:
+            arrive(11)
+            up_tiles(12, 3)
+            finish(12)
+        elif j == 14:
+            arrive(12)
+            up_tiles(15, 3)
+            finish(13)
+        elif j == 15:
+            arrive(13)
+            down(0, tile)
+            finish(14)
+        elif j == 16:
+            arrive(14)
+            down(tile, tile)
+            finish(15)
             ready(15)
-            down_pieces(4, 2)
-        if j == 17:
+            down(2 * tile, tile)
+        elif j == 17:
+            finish(16)
             ready(16)
-            down_pieces(6, 1)
-        if j == 18:
+            down(3 * tile, tile, 0, halves // 2)
+        elif j == 18:
+            down(3 * tile, tile, halves // 2, halves)
+            finish(17)
             ready(17)
-            down_pieces(8, 1)
-        if j == 19:
+            down(4 * tile, tile, 0, halves // 2)
+        elif j == 19:
+            down(4 * tile, tile, halves // 2, halves)
+            finish(18)
             finish(19)
             ready(18)
-            down_pieces(10, 1)
+            down(5 * tile, tile // 2)
             ready(19)
-            down_pieces(11, 1)
+            down(5 * tile + tile // 2, tile // 2)
+        elif j == 1:
+            finish(0)
 
     for j in range(n_blk):
         stage(j)
@@ -477,7 +499,7 @@
         scratch_shapes=[
             vmem((seq, d_model), BF16), vmem((seq, d_model), BF16), vmem((nq // HEAD_DIM, seq, HEAD_DIM), BF16),
             vmem((nkv // HEAD_DIM, seq, HEAD_DIM), BF16), vmem((nkv // HEAD_DIM, seq, HEAD_DIM), BF16), vmem((seq, ff), BF16),
-            vmem((2, side, side, 2, share, tile), BF16), vmem((2, side, 2, wd.shape[0], tile // 2), BF16), vmem((seq, tile // 2), F32),
+            vmem((2, side, side, 2, share, tile), BF16), vmem((2, side, 2, wd.shape[0], tile), BF16), vmem((seq, tile), F32),
             vmem((seq, HEAD_DIM), F32), vmem((seq, HEAD_DIM), F32), vmem((seq, nkv // HEAD_DIM, HEAD_DIM), BF16),
             vmem((ln_part.shape[0], d_model), F32), vmem((side, side, 2, ln_part.shape[0], 2 * LANES), F32), vmem(ln_part.shape, F32),
             pltpu.SemaphoreType.DMA((len(blocks), 5)), pltpu.SemaphoreType.DMA((len(blocks), 5)),

time: 485 us -> 473 us (0.975)
  Pallas kernels: 471 us -> 459 us
    pallas_call x1, Pallas kernels: 471 us -> 459 us  [run_layer(): pl.pallas_call(functools.partial(layer_kernel, cfg), out_shape=[jax.Shape...]
where the time goes in v3:
time: 473 us
  Pallas kernels  459 us (97%)
  local copies, waits for them, and re-layouts  9.27 us (2%)
    pallas_call x1, Pallas kernels, run_layer(): pl.pallas_call(functools.partial(layer_kernel, cfg), out_shape=[jax.Shape...  459 us

profile of v3, /device:TPU:97, one launch (start us, length us, event | category | flops | bytes accessed | tf_op | source)
XLA Modules:
  0.0 472.6 jit_solution(12525846044492333080)
XLA Ops:
  1.3 0.7 pad_maximum_fusion
  2.0 0.7 convert_element_type.4
  2.7 0.5 dynamic_update_slice.3.ln_ref
  3.2 0.0 copy-start.2
  3.2 1.3 multiply_sine_fusion
  4.5 0.0 copy-done.2
  4.5 459.3 %shard_map.148 = (bf16[1024,3072]{1,0:T(8,128)(2,1)}, bf16[1024,8,128]{2,1,0:T(8,128)(2,1)}, bf16[1024,8,128]{2,1,0:T(8,128)(2,1)}, f32[4,4,2,8,512]{4,3,2,1,0:T...) custom-call(s32[1]{0:T(128)S(6)} %copy.20.len_ref, ...), custom_call_target="tpu_custom_call" | custom-call | flops 167503724544 | bytes 113246208 | tf_op jit(solution)/shard_map/pallas_call | solution.py:492
  463.8 0.0 copy-start.1
  463.9 0.0 copy-start
  463.9 6.1 %copy.21 = bf16[1,1024,3072]{2,1,0:T(8,128)(2,1)} copy(bf16[1,1024,3072]{2,1,0:T(8,128)(2,1)} %bitcast.9) | data formatting | bytes 12582912
  470.0 0.0 copy-done.1
  470.0 1.3 copy.22
  471.3 0.0 copy-done
  471.3 1.3 copy.23
  (2 shorter events, 0.0 us)
Async XLA Ops:
  3.2 1.3 copy-start.2
  463.8 6.1 %copy-start.1 = (bf16[1024,8,128]{2,1,0:T(8,128)(2,1)S(1)}, bf16[1024,8,128]{2,1,0:T(8,128)(2,1)}, u32[]{:S(2)}) copy-start(bf16[1024,8,128]{2,1,0:T(8,128)(2,1)} %get-tuple-element.7) | copy-start | bytes 6291460
  463.9 7.4 %copy-start = (bf16[1024,8,128]{2,1,0:T(8,128)(2,1)S(1)}, bf16[1024,8,128]{2,1,0:T(8,128)(2,1)}, u32[]{:S(2)}) copy-start(bf16[1024,8,128]{2,1,0:T(8,128)(2,1)} %get-tuple-element.8) | copy-start | bytes 6291460

commit v4 on v3

--- a/solution.py
+++ b/solution.py
@@ -252,14 +252,15 @@
 
         matmul_tiles(gu, first, count, epilogue)
 
-    def down(col0, width, m_lo=0, m_hi=seq // rows_m):
+    def down(col0, width, m_lo=0, m_hi=seq // rows_m, primed=False, prime=False):
         cols, wide = pl.ds(col0, width), pl.ds(0, width)
         depth = a_s.shape[1] // side
 
         def fetch(k, slot):
             return pltpu.make_async_copy(gd.at[k, :, :, :, cols], wbd.at[slot, :, :, :, wide], wbd_sem.at[slot])
 
-        fetch(0, 0).start()
+        if not primed:
+            fetch(0, 0).start()
 
         @pl.loop(0, side)
         def _(k):
@@ -268,6 +269,11 @@
             @pl.when(k + 1 < side)
             def _():
                 fetch(k + 1, lax.rem(k + 1, 2)).start()
+
+            if prime:
+                @pl.when(k + 1 == side)
+                def _():
+                    fetch(0, 0).start()
 
             fetch(k, slot).wait()
             deep = pl.ds(pl.multiple_of(k * depth, LANES), depth)
@@ -445,20 +451,18 @@
         elif j == 17:
             finish(16)
             ready(16)
-            down(3 * tile, tile, 0, halves // 2)
+            down(3 * tile, tile, 0, halves // 2, prime=True)
         elif j == 18:
-            down(3 * tile, tile, halves // 2, halves)
+            down(3 * tile, tile, halves // 2, halves, primed=True)
             finish(17)
+        elif j == 19:
             ready(17)
-            down(4 * tile, tile, 0, halves // 2)
-        elif j == 19:
-            down(4 * tile, tile, halves // 2, halves)
+            down(4 * tile, tile, 0, halves // 2, prime=True)
             finish(18)
             finish(19)
-            ready(18)
-            down(5 * tile, tile // 2)
-            ready(19)
-            down(5 * tile + tile // 2, tile // 2)
+            down(4 * tile, tile, halves // 2, halves, primed=True)
+            arrive(18, 19)
+            down(5 * tile, tile)
         elif j == 1:
             finish(0)
 

time: 473 us -> 468 us (0.989)
  Pallas kernels: 459 us -> 454 us
    pallas_call x1, Pallas kernels: 459 us -> 454 us  [run_layer(): pl.pallas_call(functools.partial(layer_kernel, cfg), out_shape=[jax.Shape...]
where the time goes in v4:
time: 468 us; the launch traced here: 467 us
  Pallas kernels  454 us (97%)
  local copies, waits for them, and re-layouts  9.27 us (2%)
    pallas_call x1, Pallas kernels, run_layer(): pl.pallas_call(functools.partial(layer_kernel, cfg), out_shape=[jax.Shape...  454 us

profile of v4, /device:TPU:97, one launch (start us, length us, event | category | flops | bytes accessed | tf_op | source)
XLA Modules:
  0.0 467.4 jit_solution(18093344832569105218)
XLA Ops:
  1.3 0.7 pad_maximum_fusion
  2.0 0.7 convert_element_type.4
  2.7 0.5 dynamic_update_slice.3.ln_ref
  3.2 0.0 copy-start.2
  3.2 1.3 multiply_sine_fusion
  4.5 0.0 copy-done.2
  4.5 454.1 %shard_map.148 = (bf16[1024,3072]{1,0:T(8,128)(2,1)}, bf16[1024,8,128]{2,1,0:T(8,128)(2,1)}, bf16[1024,8,128]{2,1,0:T(8,128)(2,1)}, f32[4,4,2,8,512]{4,3,2,1,0:T...) custom-call(s32[1]{0:T(128)S(6)} %copy.20.len_ref, ...), custom_call_target="tpu_custom_call" | custom-call | flops 167503724544 | bytes 113246208 | tf_op jit(solution)/shard_map/pallas_call | solution.py:496
  458.6 0.0 copy-start.1
  458.6 0.0 copy-start
  458.6 6.1 %copy.21 = bf16[1,1024,3072]{2,1,0:T(8,128)(2,1)} copy(bf16[1,1024,3072]{2,1,0:T(8,128)(2,1)} %bitcast.9) | data formatting | bytes 12582912
  464.7 0.0 copy-done.1
  464.8 1.3 copy.22
  466.1 0.0 copy-done
  466.1 1.3 copy.23
  (2 shorter events, 0.0 us)
Async XLA Ops:
  3.2 1.3 copy-start.2
  458.6 6.1 %copy-start.1 = (bf16[1024,8,128]{2,1,0:T(8,128)(2,1)S(1)}, bf16[1024,8,128]{2,1,0:T(8,128)(2,1)}, u32[]{:S(2)}) copy-start(bf16[1024,8,128]{2,1,0:T(8,128)(2,1)} %get-tuple-element.7) | copy-start | bytes 6291460
  458.6 7.4 %copy-start = (bf16[1024,8,128]{2,1,0:T(8,128)(2,1)S(1)}, bf16[1024,8,128]{2,1,0:T(8,128)(2,1)}, u32[]{:S(2)}) copy-start(bf16[1024,8,128]{2,1,0:T(8,128)(2,1)} %get-tuple-element.8) | copy-start | bytes 6291460
